TPU v7x, 32 devices: a whole 2x2x4 slice. The times are simulated.
32 devices in a mesh: blk: 8 (over y, x, core), row: 4 (over z).
Axes of the slice: x: 2, y: 2, z: 4, core: 2. Of those that a mesh axis runs over, the one named last changes fastest.
Arguments:
- rank_start: float32 [512, 128], P(('blk', 'row')), may hold values from 0.5 to 1.5
- tiles: bfloat16 [1024, 128, 128], P(('blk', 'row')), may hold values from 0 to 1
- tile_dest: int32 [1024], P(('blk', 'row')), may hold values from 0 to 63
- tile_src: int32 [1024], P(('blk', 'row')), may hold values from 0 to 127
- tile_fill: int32 [1024], P(('blk', 'row')), may hold values from 0 to 128
- out_degree: int32 [512, 128], P(('blk', 'row')), may hold values from 64 to 255
- dangling: int32 [512, 128], P(('blk', 'row')), may hold values 0 or 1
Outputs:
- rank: float32 [512, 128], P(('blk', 'row'))
- changes: float32 [2], replicated
Inputs may be any that keep to these rules, and one draw needn't show every extreme that they name: `tile_fill`: 0 marks an empty slot.
All inputs are finite; a program needn't handle non-finite values. No bound on the sum of `dangling` on one device may be relied on, other than what follows from the above.
Results may differ from a plain program's by a relative error of at most 0.0003.
Values may be sent and summed in bfloat16 or wider, within the bound.
No kernel may reach another device: no remote copies, remote signals or barrier semaphores. Data moves between devices by JAX's collectives and lax.ppermute only.
A program may use at most 64 MiB of HBM per device.

v0:
```python
import jax
import jax.numpy as jnp
from jax import lax
from jax.sharding import PartitionSpec as P

ITERS = 2


damping = 0.85


def local(rank_start, tiles, tile_dest, tile_src, tile_fill, out_degree, dangling):
    share_tiles = rank_start.shape[0]
    page_total = lax.axis_size("blk") * lax.axis_size("row") * share_tiles * 128
    lane_index = jnp.arange(128, dtype=jnp.int32)
    column_mask = lane_index[None, :] < tile_fill[:, None]
    dangle = dangling.astype(jnp.float32)
    weight = (1.0 - dangle) / out_degree.astype(jnp.float32)
    rank = rank_start
    lost_mass = lax.psum(jnp.sum(rank * dangle), ("blk", "row"))
    change_list = []
    for iteration in range(ITERS):
        if iteration > 0:
            lost_mass = lax.psum(jnp.sum(rank * dangle), ("blk", "row"))
        scaled = (rank * weight).astype(jnp.bfloat16)
        block_part = lax.all_gather(scaled, "blk", axis=0, tiled=True)
        select = (
            tile_src[:, None] == jnp.arange(block_part.shape[0], dtype=jnp.int32)[None, :]
        ).astype(jnp.bfloat16)
        picked = jnp.dot(select, block_part, preferred_element_type=jnp.float32)
        sources = picked.astype(jnp.bfloat16)
        sources = jnp.where(column_mask, sources, jnp.zeros_like(sources))
        products = jnp.einsum("kij,kj->ki", tiles, sources, preferred_element_type=jnp.float32)
        dest_select = (
            tile_dest[:, None]
            == jnp.arange(lax.axis_size("row") * share_tiles, dtype=jnp.int32)[None, :]
        ).astype(jnp.float32)
        incoming = lax.psum_scatter(
            jnp.einsum("kd,ki->di", dest_select, products, precision=lax.Precision.HIGHEST),
            "row",
            scatter_dimension=0,
            tiled=True,
        )
        updated = damping * incoming + (1.0 - damping) + damping * lost_mass / page_total
        local_change = jnp.sum(jnp.abs(updated - rank))
        total_change = lax.psum(local_change, ("blk", "row"))
        change_list.append(total_change)
        rank = updated
    return (rank, jnp.stack(change_list))


def solution(mesh):
    placed = (
        P(("blk", "row"), None),
        P(("blk", "row"), None, None),
        P(("blk", "row")),
        P(("blk", "row")),
        P(("blk", "row")),
        P(("blk", "row"), None),
        P(("blk", "row"), None),
    )
    return jax.shard_map(
        local, mesh=mesh, in_specs=placed, out_specs=(P(("blk", "row"), None), P()), check_vma=False
    )
```

profile of v0, /device:TPU:0, one launch (start us, length us, event | category | flops | bytes accessed | tf_op | source)
XLA Modules:
  0.0 166.6 jit_solution(10766584483716675937)
XLA Ops:
  7.2 0.0 copy-start
  7.2 0.0 reduce-scatter.3.cloned.1.call-start
  7.2 1.4 multiply_convert_fusion.1
  8.6 0.0 copy-start.5
  8.6 0.0 copy-start.6
  8.6 10.7 %all_gather.6 = bf16[128,128]{1,0:T(8,128)(2,1)S(1)} all-gather(bf16[16,128]{1,0:T(8,128)(2,1)S(1)} %get-tuple-element.9), channel_id=1, replica_groups=mesh['blk'=8,'row'=4] {'blk'}, dimensions={0}, use_global_device_ids=true | all-gather | bytes 36864 | tf_op jit(solution)/shard_map/all_gather | solution.py:26
  19.4 0.0 copy-done.5
  19.4 0.0 copy-done.6
  19.4 0.2 fusion.1
  19.6 0.0 copy-done
  19.6 0.6 fusion.6
  20.2 0.0 copy-start.7
  20.2 0.7 copy-done.7
  20.9 0.9 fusion.9
  21.8 0.0 copy-start.1
  21.8 0.0 copy-start.2
  21.8 0.0 copy-start.3
  21.8 0.0 reduce-scatter.3.cloned.1.call-update
  21.8 0.0 reduce-scatter.5.cloned.1.call-start
  21.8 39.8 %psum.28 = f32[]{:T(128)} all-reduce(f32[]{:T(128)} %get-tuple-element.10), channel_id=1, replica_groups=mesh['blk'=8,'row'=4] {'blk','row'}, use_global_device_ids=true, to_apply=%region_2.3 | all-reduce | flops 1 | bytes 8 | tf_op jit(solution)/shard_map/psum | solution.py:20
  62.3 0.0 reduce-scatter.3.cloned.1.call-done
  62.3 0.0 copy-done.1
  62.3 0.0 copy-done.2
  62.4 0.0 copy-done.3
  62.4 1.3 abs_reduce_fusion.1
  63.7 10.1 %all_gather.7 = bf16[128,128]{1,0:T(8,128)(2,1)S(1)} all-gather(bf16[16,128]{1,0:T(8,128)(2,1)S(1)} %get-tuple-element.8), channel_id=1, replica_groups=mesh['blk'=8,'row'=4] {'blk'}, dimensions={0}, use_global_device_ids=true | all-gather | bytes 36864 | tf_op jit(solution)/shard_map/all_gather | solution.py:26
  73.7 0.2 fusion.3
  73.9 0.6 fusion.4
  74.6 0.9 fusion.8
  75.5 0.0 copy-start.4
  75.5 0.0 reduce-scatter.5.cloned.1.call-update
  75.5 39.5 %psum.29 = f32[]{:T(128)} all-reduce(f32[]{:T(128)} %get-tuple-element.3), channel_id=1, replica_groups=mesh['blk'=8,'row'=4] {'blk','row'}, use_global_device_ids=true, to_apply=%region_5.6 | all-reduce | flops 1 | bytes 8 | tf_op jit(solution)/shard_map/psum | solution.py:24
  115.6 0.0 reduce-scatter.5.cloned.1.call-done
  115.6 0.0 copy-done.4
  115.7 2.0 %abs_reduce_fusion = (f32[]{:T(128)}, f32[16,128]{1,0:T(8,128)}) fusion(f32[]{:T(128)S(6)} %div.10, f32[16,128]{1,0:T(8,128)S(1)} %copy-done.4, f32[]{:T(128)S(6)} %div.11, f32[16,128]{1,0:T(8,128)} %reduce-scatter.5.cloned.1.call-done), kind=kLoop, calls=%fused_computation.15 | loop fusion | flops 18431 | bytes 24588 | tf_op jit(solution)/shard_map/reduce_sum | solution.py:45
  117.6 40.4 %all-reduce = (f32[1]{0:T(128)}, f32[1]{0:T(128)}) all-reduce(f32[1]{0:T(128)} %bitcast.7, f32[1]{0:T(128)} %bitcast.6), channel_id=1, replica_groups=mesh['blk'=8,'row'=4] {'blk','row'}, use_global_device_ids=true, to_apply=%region_9.10 | all-reduce | flops 2 | bytes 16 | tf_op jit(solution)/shard_map/psum | solution.py:46
  158.0 1.8 %pad_maximum_fusion = f32[2]{0:T(128)} fusion(f32[1]{0:T(128)} %get-tuple-element.4, f32[1]{0:T(128)} %get-tuple-element.5), kind=kLoop, calls=%fused_computation.28 | loop fusion | flops 2 | bytes 16 | tf_op jit(solution)/shard_map/stack | solution.py:49
Async XLA Ops:
  7.2 12.4 %copy-start = (bf16[32,128,128]{2,1,0:T(8,128)(2,1)S(1)}, bf16[32,128,128]{2,1,0:T(8,128)(2,1)}, u32[]{:S(2)}) copy-start(bf16[32,128,128]{2,1,0:T(8,128)(2,1)} %param.8) | copy-start | bytes 3145732
  7.2 55.1 %reduce-scatter.3.cloned.1.call-start = ((), (), s32[]{:S(2)}) async-start(), calls=%async_computation.2 | async-start | bytes 40960 | tf_op jit(solution)/shard_map/reduce_scatter | solution.py:38
  8.6 10.7 %copy-start.5 = (s32[32]{0:T(128)S(1)}, s32[32]{0:T(128)}, u32[]{:S(2)}) copy-start(s32[32]{0:T(128)} %param.10) | copy-start | bytes 388
  8.6 10.7 %copy-start.6 = (s32[32]{0:T(128)S(1)}, s32[32]{0:T(128)}, u32[]{:S(2)}) copy-start(s32[32]{0:T(128)} %param.11) | copy-start | bytes 388
  20.2 0.7 copy-start.7
  21.8 40.6 %copy-start.1 = (f32[16,128]{1,0:T(8,128)S(1)}, f32[16,128]{1,0:T(8,128)}, u32[]{:S(2)}) copy-start(f32[16,128]{1,0:T(8,128)} %param.7) | copy-start | bytes 24580
  21.8 40.6 %copy-start.2 = (s32[16,128]{1,0:T(8,128)S(1)}, s32[16,128]{1,0:T(8,128)}, u32[]{:S(2)}) copy-start(s32[16,128]{1,0:T(8,128)} %param.12) | copy-start | bytes 24580
  21.8 40.6 %copy-start.3 = (s32[16,128]{1,0:T(8,128)S(1)}, s32[16,128]{1,0:T(8,128)}, u32[]{:S(2)}) copy-start(s32[16,128]{1,0:T(8,128)} %param.13) | copy-start | bytes 24580
  21.8 93.8 %reduce-scatter.5.cloned.1.call-start = ((), (), s32[]{:S(2)}) async-start(), calls=%async_computation.3 | async-start | bytes 40960 | tf_op jit(solution)/shard_map/reduce_scatter | solution.py:38
  75.5 40.2 %copy-start.4 = (f32[16,128]{1,0:T(8,128)S(1)}, f32[16,128]{1,0:T(8,128)}, u32[]{:S(2)}) copy-start(f32[16,128]{1,0:T(8,128)} %reduce-scatter.3.cloned.1.call-done) | copy-start | bytes 24580
Sparse Core Ops, SparseCore 0:
  21.9 19.4 reduce-scatter.2
  75.6 18.2 reduce-scatter.4
where the time goes:
time: 168 us; the launch traced here: 167 us
  blocking collectives  140 us (83%)
  between operations  15.4 us (9%)
  other arithmetic  6.49 us (4%)
  matrix products  3.45 us (2%)
    psum x2, blocking collectives, local(): lost_mass = lax.psum(jnp.sum(rank * dangle), ('blk', 'row'))  79.3 us
    psum x1, blocking collectives, local(): total_change = lax.psum(local_change, ('blk', 'row'))  40.4 us
    all_gather x2, blocking collectives, local(): block_part = lax.all_gather(scaled, 'blk', axis=0, tiled=True)  20.8 us
  transfers between devices with their start and end apart: 2, of which 0 were waited for; matrix products, arithmetic and copies ran while one was open for 0% of the time, Pallas kernels for 0%

commit v1 on v0

v1 whole, which is shorter than its diff:
```python
import jax
import jax.numpy as jnp
from jax import lax
from jax.sharding import PartitionSpec as P

LANES = 128
SCALAR_ROWS = 8
damping = 0.85


def products_of(scaled, tiles, tile_dest, tile_src, column_mask, dest_tiles):
    select = (
        tile_src[:, None] == jnp.arange(scaled.shape[0], dtype=jnp.int32)[None, :]
    ).astype(jnp.bfloat16)
    picked = jnp.dot(select, scaled, preferred_element_type=jnp.float32)
    sources = picked.astype(jnp.bfloat16)
    sources = jnp.where(column_mask, sources, jnp.zeros_like(sources))
    products = jnp.einsum("kij,kj->ki", tiles, sources, preferred_element_type=jnp.float32)
    dest_select = (
        tile_dest[:, None] == jnp.arange(dest_tiles, dtype=jnp.int32)[None, :]
    ).astype(jnp.float32)
    return jnp.einsum("kd,ki->di", dest_select, products, precision=lax.Precision.HIGHEST)


def local(rank_start, tiles, tile_dest, tile_src, tile_fill, out_degree, dangling):
    share = rank_start.shape[0]
    blocks, rows = lax.axis_size("blk"), lax.axis_size("row")
    half = share // 2
    dest_tiles = rows * share
    page_total = blocks * rows * share * LANES
    b, w = lax.axis_index("blk"), lax.axis_index("row")
    core = b % 2
    column_mask = jnp.arange(LANES, dtype=jnp.int32)[None, :] < tile_fill[:, None]

    weight = (1.0 - dangling.astype(jnp.float32)) / out_degree.astype(jnp.float32)
    pack = jnp.concatenate([rank_start, weight], axis=0)
    got = lax.all_to_all(jnp.broadcast_to(pack[None], (blocks,) + pack.shape), "blk", 0, 0)
    rank0, weights = got[:, :share], got[:, share:]
    lost_here = jnp.where(weights == 0.0, 1.0, 0.0)

    scaled = (rank0 * weights).astype(jnp.bfloat16).reshape(blocks * share, LANES)
    lost0 = jnp.sum(rank0 * lost_here)
    part = products_of(scaled, tiles, tile_dest, tile_src, column_mask, dest_tiles)
    part = part + lost0 / page_total

    halves = part.reshape(rows, 2, half, LANES).transpose(1, 0, 2, 3)
    send = jnp.broadcast_to(halves[None], (blocks // 2,) + halves.shape)
    send = send.reshape(blocks * rows, half, LANES)
    got = lax.all_to_all(send, ("blk", "row"), 0, 0)
    mine = damping * jnp.sum(got.reshape(blocks, rows, half, LANES), axis=1) + (1.0 - damping)
    other = lax.ppermute(mine, "blk", [(i, i ^ 1) for i in range(blocks)])
    low = jnp.where(core == 0, mine, other)
    high = jnp.where(core == 0, other, mine)
    rank1 = jnp.concatenate([low, high], axis=1)

    change0 = jnp.sum(jnp.abs(rank1 - rank0))
    lost1 = jnp.sum(rank1 * lost_here)
    scaled = (rank1 * weights).astype(jnp.bfloat16).reshape(blocks * share, LANES)
    part = products_of(scaled, tiles, tile_dest, tile_src, column_mask, dest_tiles)
    part = damping * (part + lost1 / page_total)
    own = lax.dynamic_index_in_dim(rank1, b, 0, keepdims=False)
    is_own = (jnp.arange(rows) == w)[:, None, None]
    part = part.reshape(rows, share, LANES)
    less = jnp.where(is_own, part - (own - (1.0 - damping))[None], part)

    pack = jnp.concatenate(
        [less.reshape(dest_tiles, LANES), jnp.broadcast_to(change0, (SCALAR_ROWS, LANES))], axis=0
    )
    got = lax.all_to_all(jnp.broadcast_to(pack[None], (rows,) + pack.shape), "row", 0, 0)
    change1 = jnp.sum(jnp.abs(jnp.sum(got[:, :dest_tiles], axis=0)))
    change0 = jnp.sum(got[:, dest_tiles, 0])
    theirs = lax.dynamic_slice_in_dim(got, w * share, share, 1)
    own_part = lax.dynamic_index_in_dim(part, w, 0, keepdims=False)
    rank2 = jnp.sum(jnp.where(is_own, own_part[None], theirs), axis=0) + (1.0 - damping)

    got = lax.all_to_all(jnp.broadcast_to(change1, (blocks, 1, LANES)), "blk", 0, 0)
    change1 = jnp.sum(got[:, 0, 0])
    return rank2, jnp.stack([change0, change1])


def solution(mesh):
    placed = (
        P(("blk", "row"), None),
        P(("blk", "row"), None, None),
        P(("blk", "row")),
        P(("blk", "row")),
        P(("blk", "row")),
        P(("blk", "row"), None),
        P(("blk", "row"), None),
    )
    return jax.shard_map(
        local, mesh=mesh, in_specs=placed, out_specs=(P(("blk", "row"), None), P()), check_vma=False
    )
```

time: 168 us -> 56.6 us (0.34)
  blocking collectives: 140 us -> 10.5 us
  waiting for transfers between devices: 0.08 us -> 19.3 us
  between operations: 15.4 us -> 2.15 us
  starting transfers between devices: 0.08 us -> 10.7 us
  local copies, waits for them, and re-layouts: 0.71 us -> 4.72 us
    psum x3 -> x0, blocking collectives: 120 us -> none  [the longest x2 79.3 us: local(): lost_mass = lax.psum(jnp.sum(rank * dangle), ('blk', 'row'))]
    all_gather x2 -> x0, blocking collectives: 20.8 us -> none  [local(): block_part = lax.all_gather(scaled, 'blk', axis=0, tiled=True)]
    all_to_all x0 -> x3, waiting for transfers between devices: none -> 18.3 us  [the longest x1 8.37 us: local(): got = lax.all_to_all(send, ('blk', 'row'), 0, 0)]
    all_to_all x0 -> x3, starting transfers between devices: none -> 10.6 us  [the longest x1 3.97 us: local(): got = lax.all_to_all(send, ('blk', 'row'), 0, 0)]
    all_to_all x0 -> x1, blocking collectives: none -> 10.5 us  [local(): lax.all_to_all(jnp.broadcast_to(pack[None], (blocks,) + pack.shape), 'blk...]
    broadcast_in_dim x0 -> x7, local copies, waits for them, and re-layouts: none -> 2.73 us  [the longest x1 1.24 us: local(): jnp.broadcast_to(change1, (blocks, 1, LANES))]
  transfers between devices with their start and end apart: 2 -> 4, of which waited for: 0 -> 4; matrix products, arithmetic and copies ran while one was open for 0% -> 3% of each run, Pallas kernels for 0% -> 0%
where the time goes in v1:
time: 56.6 us; the launch traced here: 56.1 us
  waiting for transfers between devices  19.3 us (34%)
  starting transfers between devices  10.7 us (19%)
  blocking collectives  10.5 us (19%)
  other arithmetic  6.52 us (12%)
  local copies, waits for them, and re-layouts  4.72 us (8%)
  matrix products  2.23 us (4%)
  between operations  2.15 us (4%)
    all_to_all x1, blocking collectives, local(): lax.all_to_all(jnp.broadcast_to(pack[None], (blocks,) + pack.shape), 'blk...  10.5 us
    all_to_all x1, waiting for transfers between devices, local(): got = lax.all_to_all(send, ('blk', 'row'), 0, 0)  8.37 us
    all_to_all x1, waiting for transfers between devices, local(): lax.all_to_all(jnp.broadcast_to(pack[None], (rows,) + pack.shape), 'row',...  6.59 us
    all_to_all x1, starting transfers between devices, local(): got = lax.all_to_all(send, ('blk', 'row'), 0, 0)  3.97 us
    all_to_all x1, starting transfers between devices, local(): lax.all_to_all(jnp.broadcast_to(pack[None], (rows,) + pack.shape), 'row',...  3.33 us
    all_to_all x1, starting transfers between devices, local(): lax.all_to_all(jnp.broadcast_to(change1, (blocks, 1, LANES)), 'blk', 0, 0)  3.33 us
    all_to_all x1, waiting for transfers between devices, local(): lax.all_to_all(jnp.broadcast_to(change1, (blocks, 1, LANES)), 'blk', 0, 0)  3.33 us
    another operation x1, other arithmetic, local(): return (rank2, jnp.stack([change0, change1]))  1.83 us
  transfers between devices with their start and end apart: 4, of which 4 were waited for; matrix products, arithmetic and copies ran while one was open for 3% of the time, Pallas kernels for 0%

profile of v1, /device:TPU:0, one launch (start us, length us, event | category | flops | bytes accessed | tf_op | source)
XLA Modules:
  0.0 56.1 jit_solution(14962860932366040095)
XLA Ops:
  0.6 0.0 copy-start
  0.6 0.0 copy-start.1
  0.7 0.8 %convert_divide_fusion = f32[16,128]{1,0:T(8,128)S(1)} fusion(s32[16,128]{1,0:T(8,128)} %param.12, s32[16,128]{1,0:T(8,128)} %param.13), kind=kLoop, calls=%fused_computation.40 | loop fusion | flops 8192 | bytes 24576 | tf_op jit(solution)/shard_map/div | solution.py:35
  1.5 0.0 copy-done.1
  1.5 10.5 %all_to_all.20 = f32[8,32,128]{2,1,0:T(8,128)S(1)} all-to-all(f32[8,32,128]{2,1,0:T(8,128)S(1)} %broadcast_in_dim.39), channel_id=1, replica_groups=mesh['blk'=8,'row'=4] {'blk'}, dimensions={0} | all-to-all | bytes 262144 | tf_op jit(solution)/shard_map/all_to_all | solution.py:37
  12.0 0.6 %fusion.5 = (f32[]{:T(128)}, pred[8,16,128]{2,1,0:T(8,128)(4,1)S(1)}, bf16[8,16,128]{2,1,0:T(8,128)(2,1)S(1)}) fusion(f32[8,32,128]{2,1,0:T(8,128)S(1)} %all_to_all.20), kind=kLoop, calls=%fused_computation.16 | loop fusion | flops 98303 | bytes 180228 | tf_op jit(solution)/shard_map/reduce_sum | solution.py:42
  12.6 0.0 copy-start.3
  12.6 0.0 copy-start.4
  12.6 0.7 %copy-done.3 = s32[32]{0:T(128)S(1)} copy-done((s32[32]{0:T(128)S(1)}, s32[32]{0:T(128)}, u32[]{:S(2)}) %copy-start.3) | copy-done | bytes 152
  13.3 0.0 copy-done.4
  13.3 0.2 fusion.2
  13.5 0.0 copy-done
  13.5 0.6 %fusion.9 = f32[32,1,128]{2,1,0:T(1,128)S(1)} fusion(bf16[32,128,128]{2,1,0:T(8,128)(2,1)S(1)} %copy-done, bf16[32,128,1]{1,0,2:T(8,128)(2,1)S(1)} %fusion.2), kind=kOutput, calls=%fused_computation.29 | convolution fusion | flops 1048576 | bytes 1073152 | tf_op jit(solution)/shard_map/kij,kj->ki/dot_general | solution.py:18
  14.8 0.0 copy-start.2
  14.8 0.6 %copy-done.2 = s32[32]{0:T(128)S(1)} copy-done((s32[32]{0:T(128)S(1)}, s32[32]{0:T(128)}, u32[]{:S(2)}) %copy-start.2) | copy-done | bytes 152
  15.4 0.3 convolution_add_fusion.1
  15.7 0.6 %broadcast_in_dim.41 = f32[4,2,4,8,128]{4,3,2,1,0:T(8,128)} broadcast(f32[2,4,8,128]{3,2,1,0:T(8,128)S(1)} %copy.12), dimensions={1,2,3,4} | broadcast | bytes 163840 | tf_op jit(solution)/shard_map/broadcast_in_dim | solution.py:47
  16.4 4.0 %all-to-all-start.1 = ((f32[32,8,128]{2,1,0:T(8,128)}), f32[32,8,128]{2,1,0:T(8,128)S(1)}, u32[]{:S(2)}, u32[]{:S(2)}) async-start(f32[32,8,128]{2,1,0:T(8,128)} %bitcast.6), calls=%async_computation.1 | async-start | bytes 262144 | tf_op jit(solution)/shard_map/all_to_all | solution.py:49
  20.4 8.4 %all-to-all-done.1 = f32[32,8,128]{2,1,0:T(8,128)S(1)} async-done(((f32[32,8,128]{2,1,0:T(8,128)}), f32[32,8,128]{2,1,0:T(8,128)S(1)}, u32[]{:S(2)}, u32[]{:S(2)}) %all-to-all-start.1) | async-done | bytes 131104 | tf_op jit(solution)/shard_map/all_to_all | solution.py:49
  28.8 0.1 collective-permute-start
  28.9 0.1 broadcast_in_dim.77
  29.0 0.1 broadcast_in_dim.78
  29.0 1.0 %collective-permute-done = f32[8,8,128]{2,1,0:T(8,128)S(1)} collective-permute-done((f32[8,8,128]{2,1,0:T(8,128)S(1)}, f32[8,8,128]{2,1,0:T(8,128)S(1)}, u32[]{:S(2)}, u32[]{:S(2)}) %collective-permute-start) | collective-permute-done | bytes 32800 | tf_op jit(solution)/shard_map/ppermute | solution.py:51
  30.1 0.6 %abs_reduce_fusion = (f32[]{:T(128)}, f32[]{:T(128)}, bf16[8,16,128]{2,1,0:T(8,128)(2,1)S(1)}) fusion(f32[8,32,128]{2,1,0:T(8,128)S(1)} %all_to_all.20, f32[8,8,128]{2,1,0:T(8,128)S(1)} %get-tuple-element.9, f32[8,8,128]{2,1,0:T(8,128)S(1)} %get-tuple-element.8, pred[8,16,128]{2,1,0:T(8,128)(4,1)S(1)} %get-tuple-element.5), kind=kLoop, calls=%fused_computation.18 | loop fusion | flops 147454 | bytes 245768 | tf_op jit(solution)/shard_map/reduce_sum | solution.py:56
  30.7 0.2 fusion.4
  30.9 0.6 %fusion.7 = f32[32,1,128]{2,1,0:T(1,128)S(1)} fusion(bf16[32,128,128]{2,1,0:T(8,128)(2,1)S(1)} %copy-done, bf16[32,128,1]{1,0,2:T(8,128)(2,1)S(1)} %fusion.4), kind=kOutput, calls=%fused_computation.27 | convolution fusion | flops 1048576 | bytes 1073152 | tf_op jit(solution)/shard_map/kij,kj->ki/dot_general | solution.py:18
  32.2 0.3 subtract_select_fusion
  32.5 0.7 %concatenate.11 = f32[72,128]{1,0:T(8,128)S(1)} pad(f32[64,128]{1,0:T(8,128)S(1)} %get-tuple-element.10, f32[]{:T(128)} %get-tuple-element.2), padding=0_8x0_0 | pad | bytes 69636 | tf_op jit(solution)/shard_map/concatenate | solution.py:66
  33.2 0.7 %broadcast_in_dim.80 = f32[4,72,128]{2,1,0:T(8,128)} broadcast(f32[72,128]{1,0:T(8,128)S(1)} %concatenate.11), dimensions={1,2} | broadcast | bytes 184320 | tf_op jit(solution)/shard_map/broadcast_in_dim | solution.py:69
  33.8 3.3 %all-to-all-start.2 = ((f32[4,72,128]{2,1,0:T(8,128)}), f32[4,72,128]{2,1,0:T(8,128)S(1)}, u32[]{:S(2)}, u32[]{:S(2)}) async-start(f32[4,72,128]{2,1,0:T(8,128)} %broadcast_in_dim.80), calls=%async_computation.2 | async-start | bytes 294912 | tf_op jit(solution)/shard_map/all_to_all | solution.py:69
  37.2 6.6 %all-to-all-done.2 = f32[4,72,128]{2,1,0:T(8,128)S(1)} async-done(((f32[4,72,128]{2,1,0:T(8,128)}), f32[4,72,128]{2,1,0:T(8,128)S(1)}, u32[]{:S(2)}, u32[]{:S(2)}) %all-to-all-start.2) | async-done | bytes 147488 | tf_op jit(solution)/shard_map/all_to_all | solution.py:69
  43.8 0.6 %abs_reduce_fusion.1 = f32[]{:T(128)} fusion(f32[64,128]{1,0:T(8,128)S(1)} %slice_reduce_fusion), kind=kLoop, calls=%fused_computation.23 | loop fusion | flops 16383 | bytes 32772 | tf_op jit(solution)/shard_map/reduce_sum | solution.py:70
  44.4 1.2 %broadcast_in_dim.81 = f32[8,1,128]{2,1,0:T(1,128)} broadcast(f32[]{:T(128)} %abs_reduce_fusion.1), dimensions={} | broadcast | bytes 4100 | tf_op jit(solution)/shard_map/broadcast_in_dim | solution.py:76
  45.6 3.3 %all-to-all-start.3 = ((f32[8,1,128]{2,1,0:T(1,128)}), f32[8,1,128]{2,1,0:T(1,128)S(1)}, u32[]{:S(2)}, u32[]{:S(2)}) async-start(f32[8,1,128]{2,1,0:T(1,128)} %broadcast_in_dim.81), calls=%async_computation.3 | async-start | bytes 8192 | tf_op jit(solution)/shard_map/all_to_all | solution.py:76
  49.0 0.1 select_reduce_fusion
  49.1 0.6 %broadcast_add_fusion = f32[16,128]{1,0:T(8,128)} fusion(f32[16,128]{1,0:T(8,128)S(1)} %select_reduce_fusion), kind=kLoop, calls=%fused_computation.46 | loop fusion | flops 2048 | bytes 16384 | tf_op jit(solution)/shard_map/add | solution.py:74
  49.7 0.6 %slice_reduce_fusion.2 = f32[]{:T(128)} fusion(f32[4,72,128]{2,1,0:T(8,128)S(1)} %all-to-all-done.2), kind=kLoop, calls=%fused_computation.47 | loop fusion | flops 3 | bytes 20 | tf_op jit(solution)/shard_map/reduce_sum | solution.py:71
  50.3 3.3 %all-to-all-done.3 = f32[8,1,128]{2,1,0:T(1,128)S(1)} async-done(((f32[8,1,128]{2,1,0:T(1,128)}), f32[8,1,128]{2,1,0:T(1,128)S(1)}, u32[]{:S(2)}, u32[]{:S(2)}) %all-to-all-start.3) | async-done | bytes 4128 | tf_op jit(solution)/shard_map/all_to_all | solution.py:76
  53.6 0.7 %slice_reduce_fusion.1 = f32[]{:T(128)} fusion(f32[8,1,128]{2,1,0:T(1,128)S(1)} %all-to-all-done.3), kind=kLoop, calls=%fused_computation.45 | loop fusion | flops 7 | bytes 36 | tf_op jit(solution)/shard_map/reduce_sum | solution.py:77
  54.3 1.8 %pad_maximum_fusion.2 = f32[2]{0:T(128)} fusion(f32[1]{0:T(128)} %bitcast.17, f32[1]{0:T(128)} %bitcast.16), kind=kLoop, calls=%fused_computation.48 | loop fusion | flops 2 | bytes 16 | tf_op jit(solution)/shard_map/stack | solution.py:78
  (10 shorter events, 0.1 us)
Async XLA Ops:
  0.6 12.8 %copy-start = (bf16[32,128,128]{2,1,0:T(8,128)(2,1)S(1)}, bf16[32,128,128]{2,1,0:T(8,128)(2,1)}, u32[]{:S(2)}) copy-start(bf16[32,128,128]{2,1,0:T(8,128)(2,1)} %param.8) | copy-start | bytes 3145732
  0.6 0.8 %copy-start.1 = (f32[16,128]{1,0:T(8,128)S(1)}, f32[16,128]{1,0:T(8,128)}, u32[]{:S(2)}) copy-start(f32[16,128]{1,0:T(8,128)} %param.7) | copy-start | bytes 24580
  12.6 0.7 %copy-start.3 = (s32[32]{0:T(128)S(1)}, s32[32]{0:T(128)}, u32[]{:S(2)}) copy-start(s32[32]{0:T(128)} %param.10) | copy-start | bytes 388
  12.6 0.7 %copy-start.4 = (s32[32]{0:T(128)S(1)}, s32[32]{0:T(128)}, u32[]{:S(2)}) copy-start(s32[32]{0:T(128)} %param.11) | copy-start | bytes 388
  14.8 0.7 %copy-start.2 = (s32[32]{0:T(128)S(1)}, s32[32]{0:T(128)}, u32[]{:S(2)}) copy-start(s32[32]{0:T(128)} %param.9) | copy-start | bytes 388
  16.4 12.4 %all-to-all-start.1 = ((f32[32,8,128]{2,1,0:T(8,128)}), f32[32,8,128]{2,1,0:T(8,128)S(1)}, u32[]{:S(2)}, u32[]{:S(2)}) async-start(f32[32,8,128]{2,1,0:T(8,128)} %bitcast.6), calls=%async_computation.1 | async-start | bytes 262144 | tf_op jit(solution)/shard_map/all_to_all | solution.py:49
  28.8 1.3 %collective-permute-start = (f32[8,8,128]{2,1,0:T(8,128)S(1)}, f32[8,8,128]{2,1,0:T(8,128)S(1)}, u32[]{:S(2)}, u32[]{:S(2)}) collective-permute-start(f32[8,8,128]{2,1,0:T(8,128)S(1)} %multiply_add_fusion), channel_id=1, source_target_pairs={{0,4},{4,0},{8,12},{12,8},{16,20},{20,16},{24,28},{28,24},{1,5},{5... | collective-permute-start | bytes 98312 | tf_op jit(solution)/shard_map/ppermute | solution.py:51
  33.8 10.0 %all-to-all-start.2 = ((f32[4,72,128]{2,1,0:T(8,128)}), f32[4,72,128]{2,1,0:T(8,128)S(1)}, u32[]{:S(2)}, u32[]{:S(2)}) async-start(f32[4,72,128]{2,1,0:T(8,128)} %broadcast_in_dim.80), calls=%async_computation.2 | async-start | bytes 294912 | tf_op jit(solution)/shard_map/all_to_all | solution.py:69
  45.6 8.0 %all-to-all-start.3 = ((f32[8,1,128]{2,1,0:T(1,128)}), f32[8,1,128]{2,1,0:T(1,128)S(1)}, u32[]{:S(2)}, u32[]{:S(2)}) async-start(f32[8,1,128]{2,1,0:T(1,128)} %broadcast_in_dim.81), calls=%async_computation.3 | async-start | bytes 8192 | tf_op jit(solution)/shard_map/all_to_all | solution.py:76

commit v2 on v0

v2 whole, which is shorter than its diff:
```python
import functools

import jax
import jax.numpy as jnp
from jax import lax
from jax.experimental import pallas as pl
from jax.experimental.pallas import tpu as pltpu
from jax.sharding import PartitionSpec as P

LANES = 128
SCALAR_ROWS = 8
damping = 0.85
VMEM = pl.BlockSpec(memory_space=pltpu.VMEM)
HBM = pl.BlockSpec(memory_space=pltpu.HBM)


def call(kernel, outs, scratch=(), space=VMEM):
    def run(*arguments):
        return pl.pallas_call(
            kernel,
            out_shape=outs,
            in_specs=(space,) * len(arguments),
            out_specs=(VMEM,) * len(outs) if isinstance(outs, tuple) else VMEM,
            scratch_shapes=scratch,
            compiler_params=pltpu.CompilerParams(vmem_limit_bytes=24 * 1024 * 1024),
            cost_estimate=pl.CostEstimate(flops=1000000, bytes_accessed=1000000, transcendentals=0),
        )(*arguments)

    return run


def column(row):
    n = row.shape[1]
    square = jnp.broadcast_to(row.astype(jnp.float32), (n, n))
    diagonal = lax.broadcasted_iota(jnp.int32, (n, n), 0) == lax.broadcasted_iota(jnp.int32, (n, n), 1)
    return jnp.sum(jnp.where(diagonal, square, 0.0), axis=1, keepdims=True)


def prepare(*refs):
    arguments, (payload, select, keep, dest_ids, tiles), scratch, sems = refs[:7], refs[7:12], refs[12:18], refs[18]
    copies = [
        pltpu.make_async_copy(source, target, sems.at[i])
        for i, (source, target) in enumerate(zip(arguments, (*scratch, tiles), strict=True))
    ]
    for copy in copies:
        copy.start()
    for copy in copies[:-1]:
        copy.wait()
    rank, degree, dangling, dest, src, fill = scratch
    share = rank.shape[0]
    weight = (1.0 - dangling[...].astype(jnp.float32)) / degree[...].astype(jnp.float32)
    payload[:, :share] = jnp.broadcast_to(rank[...][None], (payload.shape[0],) + rank.shape)
    payload[:, share:] = jnp.broadcast_to(weight[None], (payload.shape[0],) + rank.shape)
    lane = lax.broadcasted_iota(jnp.int32, select.shape, 1).astype(jnp.float32)
    select[...] = jnp.where(column(src[...]) == lane, 1.0, 0.0).astype(jnp.bfloat16)
    lane = lax.broadcasted_iota(jnp.int32, keep.shape, 1).astype(jnp.float32)
    keep[...] = jnp.where(lane < column(fill[...]), 1.0, 0.0)
    dest_ids[...] = jnp.broadcast_to(column(dest[...]), dest_ids.shape).astype(jnp.int32)
    copies[-1].wait()


def products(rank, weight, select, keep, dest_ids, tiles, sources, dest_tiles):
    scaled = (rank * weight).astype(jnp.bfloat16)
    picked = jnp.dot(select[...], scaled, preferred_element_type=jnp.float32)
    sources[...] = jnp.where(keep[...] > 0.0, picked, 0.0)
    target = lax.broadcasted_iota(jnp.int32, (dest_tiles, LANES), 0)
    total = jnp.zeros((dest_tiles, LANES), jnp.float32)
    for k in range(tiles.shape[0]):
        placed = jnp.where(dest_ids[pl.ds(k, 1), :] == target, sources[pl.ds(k, 1), :], 0.0)
        total += lax.dot_general(
            placed.astype(jnp.bfloat16),
            tiles[k],
            (((1,), (1,)), ((), ())),
            preferred_element_type=jnp.float32,
        )
    return total


def first(pages, rows, got, select, keep, dest_ids, tiles, send, sources):
    blocks, both, _ = got.shape
    share, half = both // 2, both // 4
    rank = got[:, :share].reshape(blocks * share, LANES)
    weight = got[:, share:].reshape(blocks * share, LANES)
    lost = jnp.sum(jnp.where(weight == 0.0, rank, 0.0))
    total = products(rank, weight, select, keep, dest_ids, tiles, sources, rows * share) + lost / pages
    for b in range(blocks):
        for w in range(rows):
            start = w * share + (b % 2) * half
            send[b * rows + w] = total[start : start + half]


def gather_rows(rows, got, mine):
    blocks = mine.shape[0]
    for b in range(blocks):
        total = got[b * rows]
        for w in range(1, rows):
            total += got[b * rows + w]
        mine[b] = damping * total + (1.0 - damping)


def second(pages, rows, mine, other, got, select, keep, dest_ids, tiles, send, own_part, sources):
    blocks, both, _ = got.shape
    share, half = both // 2, both // 4
    b, w = lax.axis_index("blk"), lax.axis_index("row")
    core0 = lax.rem(b, 2) == 0
    low = jnp.where(core0, mine[...], other[...])
    high = jnp.where(core0, other[...], mine[...])
    rank = jnp.concatenate([low, high], axis=1).reshape(blocks * share, LANES)
    rank0 = got[:, :share].reshape(blocks * share, LANES)
    weight = got[:, share:].reshape(blocks * share, LANES)
    change = jnp.sum(jnp.abs(rank - rank0))
    lost = jnp.sum(jnp.where(weight == 0.0, rank, 0.0))
    total = products(rank, weight, select, keep, dest_ids, tiles, sources, rows * share)
    total = damping * (total + lost / pages)
    own_low = jnp.where(core0, mine[b], other[b])
    own_high = jnp.where(core0, other[b], mine[b])
    own = jnp.concatenate([own_low, own_high], axis=0) - (1.0 - damping)
    kept = jnp.zeros((share, LANES), jnp.float32)
    for r in range(rows):
        piece = total[r * share : (r + 1) * share]
        kept = jnp.where(w == r, piece, kept)
        less = jnp.where(w == r, piece - own, piece)
        for to in range(rows):
            send[to, r * share : (r + 1) * share] = less
    own_part[...] = kept
    for to in range(rows):
        send[to, rows * share :] = jnp.full((SCALAR_ROWS, LANES), change, jnp.float32)


def block_change(got, send):
    rows, height, _ = got.shape
    dest_tiles = height - SCALAR_ROWS
    total = got[0]
    for r in range(1, rows):
        total += got[r]
    change1 = jnp.sum(jnp.abs(total[:dest_tiles]))
    change0 = jnp.where(lax.axis_index("blk") == 0, total[dest_tiles:, :], 0.0)[:1]
    lane = lax.broadcasted_iota(jnp.int32, (1, LANES), 1)
    line = jnp.where(lane == 0, change0, change1)
    send[...] = jnp.broadcast_to(line, send.shape)


def finish(rows, got, own_part, changes, rank, out):
    share = rank.shape[0]
    w = lax.axis_index("row")
    total = own_part[...] + (1.0 - damping)
    for r in range(rows):
        total += jnp.where(w == r, 0.0, got[r, pl.ds(w * share, share), :])
    rank[...] = total
    out[...] = jnp.sum(changes[...], axis=0)[: out.shape[0]]


def local(rank_start, tiles, tile_dest, tile_src, tile_fill, out_degree, dangling):
    share, slots = rank_start.shape[0], tiles.shape[0]
    blocks, rows = lax.axis_size("blk"), lax.axis_size("row")
    half, dest_tiles = share // 2, rows * share
    pages = float(blocks * rows * share * LANES)
    f32 = functools.partial(jax.ShapeDtypeStruct, dtype=jnp.float32)
    sources = (pltpu.VMEM((slots, LANES), jnp.float32),)

    arguments = (rank_start, out_degree, dangling, tile_dest[None], tile_src[None], tile_fill[None], tiles)
    payload, *table = call(
        prepare,
        (
            f32((blocks, 2 * share, LANES)),
            jax.ShapeDtypeStruct((slots, blocks * share), jnp.bfloat16),
            f32((slots, LANES)),
            jax.ShapeDtypeStruct((slots, LANES), jnp.int32),
            jax.ShapeDtypeStruct(tiles.shape, tiles.dtype),
        ),
        (*(pltpu.VMEM(a.shape, a.dtype) for a in arguments[:-1]), pltpu.SemaphoreType.DMA((len(arguments),))),
        HBM,
    )(*(pltpu.with_memory_space_constraint(a, pltpu.HBM) for a in arguments))

    got_a = lax.all_to_all(payload, "blk", 0, 0)
    send = call(functools.partial(first, pages, rows), f32((blocks * rows, half, LANES)), sources)(got_a, *table)

    got_b = lax.all_to_all(send, ("blk", "row"), 0, 0)
    mine = call(functools.partial(gather_rows, rows), f32((blocks, half, LANES)))(got_b)
    other = lax.ppermute(mine, "blk", [(i, i ^ 1) for i in range(blocks)])
    send, own_part = call(
        functools.partial(second, pages, rows),
        (f32((rows, dest_tiles + SCALAR_ROWS, LANES)), f32((share, LANES))),
        sources,
    )(mine, other, got_a, *table)

    got_d = lax.all_to_all(send, "row", 0, 0)
    send = call(block_change, f32((blocks, LANES)))(got_d)

    got_e = lax.all_to_all(send, "blk", 0, 0, tiled=True)
    return call(functools.partial(finish, rows), (f32((share, LANES)), f32((2,))))(got_d, own_part, got_e)


def solution(mesh):
    placed = (
        P(("blk", "row"), None),
        P(("blk", "row"), None, None),
        P(("blk", "row")),
        P(("blk", "row")),
        P(("blk", "row")),
        P(("blk", "row"), None),
        P(("blk", "row"), None),
    )
    return jax.shard_map(
        local, mesh=mesh, in_specs=placed, out_specs=(P(("blk", "row"), None), P()), check_vma=False
    )
```

time: 168 us -> 45.3 us (0.27)
  blocking collectives: 140 us -> 39.1 us
  between operations: 15.4 us -> 0.67 us
  other arithmetic: 6.49 us -> 0 us
  Pallas kernels: 0 us -> 3.94 us
  matrix products: 3.45 us -> 0 us
    psum x3 -> x0, blocking collectives: 120 us -> none  [the longest x2 79.3 us: local(): lost_mass = lax.psum(jnp.sum(rank * dangle), ('blk', 'row'))]
    all_to_all x0 -> x4, blocking collectives: none -> 39.1 us  [the longest x1 12.2 us: local(): got_b = lax.all_to_all(send, ('blk', 'row'), 0, 0)]
    all_gather x2 -> x0, blocking collectives: 20.8 us -> none  [local(): block_part = lax.all_gather(scaled, 'blk', axis=0, tiled=True)]
    pallas_call x0 -> x6, Pallas kernels: none -> 3.94 us  [run(): pl.pallas_call(kernel, out_shape=outs, in_specs=(space,) * len(arguments)...]
    dot_general x6 -> x0, matrix products: 3.45 us -> none  [the longest x2 1.8 us: local(): jnp.einsum('kd,ki->di', dest_select, products, precision=lax.Precision.HI...]
    reduce_sum x2 -> x0, other arithmetic: 3.3 us -> none  [local(): local_change = jnp.sum(jnp.abs(updated - rank))]
    another operation x1 -> x0, other arithmetic: 1.78 us -> none  [local(): return (rank, jnp.stack(change_list))]
  transfers between devices with their start and end apart: 2 -> 1, of which waited for: 0 -> 1; matrix products, arithmetic and copies ran while one was open for 0% -> 0% of each run, Pallas kernels for 0% -> 0%
where the time goes in v2:
time: 45.3 us; the launch traced here: 45 us
  blocking collectives  39.1 us (86%)
  Pallas kernels  3.94 us (9%)
  waiting for transfers between devices  1.19 us (3%)
  between operations  0.67 us (1%)
    all_to_all x1, blocking collectives, local(): got_b = lax.all_to_all(send, ('blk', 'row'), 0, 0)  12.2 us
    all_to_all x1, blocking collectives, local(): got_a = lax.all_to_all(payload, 'blk', 0, 0)  10.5 us
    all_to_all x1, blocking collectives, local(): got_d = lax.all_to_all(send, 'row', 0, 0)  9.4 us
    all_to_all x1, blocking collectives, local(): got_e = lax.all_to_all(send, 'blk', 0, 0, tiled=True)  7.05 us
    pallas_call x6, Pallas kernels, run(): pl.pallas_call(kernel, out_shape=outs, in_specs=(space,) * len(arguments)...  3.94 us
    ppermute x1, waiting for transfers between devices, local(): other = lax.ppermute(mine, 'blk', [(i, i ^ 1) for i in range(blocks)])  1.19 us
  transfers between devices with their start and end apart: 1, of which 1 were waited for; matrix products, arithmetic and copies ran while one was open for 0% of the time, Pallas kernels for 0%

profile of v2, /device:TPU:0, one launch (start us, length us, event | category | flops | bytes accessed | tf_op | source)
XLA Modules:
  0.0 45.0 jit_solution(17088780876807365560)
XLA Ops:
  0.6 1.4 %shard_map.86 = (f32[8,32,128]{2,1,0:T(8,128)S(1)}, bf16[32,128]{1,0:T(8,128)(2,1)S(1)}, f32[32,128]{1,0:T(8,128)S(1)}, s32[32,128]{1,0:T(8,128)S(1)}, bf16[32,128,128]{2,1,0:T(8,128)(2,1)S(1)}) custom-call(f32[16,128]{1,0:T(8,128)} %refs_0_.1, s32[16,128]{1,0:T(8,128)} %refs_1_.1, s32[16,128]{1,0:T(8,128)} %refs_2_.1, s32[1,32]{1,0:T(1,128)} %bitcast.9, ...), custom_call_target="tpu_custom_call" | custom-call | flops 1000000 | bytes 1000000 | tf_op jit(solution)/shard_map/pallas_call | solution.py:19
  2.0 10.5 %all_to_all.26.got = f32[8,32,128]{2,1,0:T(8,128)S(1)} all-to-all(f32[8,32,128]{2,1,0:T(8,128)S(1)} %get-tuple-element.9), channel_id=1, replica_groups=mesh['blk'=8,'row'=4] {'blk'}, dimensions={0} | all-to-all | bytes 262144 | tf_op jit(solution)/shard_map/all_to_all | solution.py:175
  12.5 0.9 %shard_map.87 = f32[32,8,128]{2,1,0:T(8,128)S(1)} custom-call(f32[8,32,128]{2,1,0:T(8,128)S(1)} %all_to_all.26.got, bf16[32,128]{1,0:T(8,128)(2,1)S(1)} %get-tuple-element.10.select, f32[32,128]{1,0:T(8,128)S(1)} %get-tuple-element.11.keep, s32[32,128]{1,0:T(8,128)S(1)} %get-tuple-element.12.dest_ids, bf16[32,128,128]{2,1,0:T(8,128)(2,1)S(1)} %get-tuple-element.13.tiles), custom_call_target="tpu_custom_call" | custom-call | flops 1000000 | bytes 1000000 | tf_op jit(solution)/shard_map/pallas_call | solution.py:19
  13.4 12.2 %all_to_all.27.got = f32[32,8,128]{2,1,0:T(8,128)S(1)} all-to-all(f32[32,8,128]{2,1,0:T(8,128)S(1)} %shard_map.87), channel_id=1, replica_groups=mesh['blk'=8,'row'=4] {'blk','row'}, dimensions={0} | all-to-all | bytes 262144 | tf_op jit(solution)/shard_map/all_to_all | solution.py:178
  25.6 0.1 collective-permute-start
  25.7 1.2 %collective-permute-done.other = f32[8,8,128]{2,1,0:T(8,128)S(1)} collective-permute-done((f32[8,8,128]{2,1,0:T(8,128)S(1)}, f32[8,8,128]{2,1,0:T(8,128)S(1)}, u32[]{:S(2)}, u32[]{:S(2)}) %collective-permute-start) | collective-permute-done | bytes 32800 | tf_op jit(solution)/shard_map/ppermute | solution.py:180
  26.9 0.9 %shard_map.89 = (f32[4,72,128]{2,1,0:T(8,128)S(1)}, f32[16,128]{1,0:T(8,128)S(1)}) custom-call(f32[8,8,128]{2,1,0:T(8,128)S(1)} %shard_map.88.mine, f32[8,8,128]{2,1,0:T(8,128)S(1)} %collective-permute-done.other, f32[8,32,128]{2,1,0:T(8,128)S(1)} %all_to_all.26.got, bf16[32,128]{1,0:T(8,128)(2,1)S(1)} %get-tuple-element.10.select, ...), custom_call_target="tpu_custom_call" | custom-call | flops 1000000 | bytes 1000000 | tf_op jit(solution)/shard_map/pallas_call | solution.py:19
  27.8 9.4 %all_to_all.28.got = f32[4,72,128]{2,1,0:T(8,128)S(1)} all-to-all(f32[4,72,128]{2,1,0:T(8,128)S(1)} %get-tuple-element.14), channel_id=1, replica_groups=mesh['blk'=8,'row'=4] {'row'}, dimensions={0} | all-to-all | bytes 294912 | tf_op jit(solution)/shard_map/all_to_all | solution.py:187
  37.2 0.1 shard_map.90
  37.3 7.1 %all_to_all.29 = f32[8,1,128]{2,1,0:T(1,128)S(1)} all-to-all(f32[8,1,128]{2,1,0:T(1,128)S(1)} %bitcast.8), channel_id=1, replica_groups=mesh['blk'=8,'row'=4] {'blk'}, dimensions={0} | all-to-all | bytes 8192 | tf_op jit(solution)/shard_map/all_to_all | solution.py:190
  44.4 0.6 %shard_map.91 = (f32[16,128]{1,0:T(8,128)}, f32[2]{0:T(128)}) custom-call(f32[4,72,128]{2,1,0:T(8,128)S(1)} %all_to_all.28.got, f32[16,128]{1,0:T(8,128)S(1)} %get-tuple-element.15.own_part, f32[8,128]{1,0:T(8,128)S(1)} %bitcast.7), custom_call_target="tpu_custom_call" | custom-call | flops 1000000 | bytes 1000000 | tf_op jit(solution)/shard_map/pallas_call | solution.py:19
  (1 shorter events, 0.0 us)
Async XLA Ops:
  25.6 1.3 %collective-permute-start = (f32[8,8,128]{2,1,0:T(8,128)S(1)}, f32[8,8,128]{2,1,0:T(8,128)S(1)}, u32[]{:S(2)}, u32[]{:S(2)}) collective-permute-start(f32[8,8,128]{2,1,0:T(8,128)S(1)} %shard_map.88.mine), channel_id=1, source_target_pairs={{0,4},{4,0},{8,12},{12,8},{16,20},{20,16},{24,28},{28,24},{1,5},{5... | collective-permute-start | bytes 98312 | tf_op jit(solution)/shard_map/ppermute | solution.py:180

commit v3 on v2

--- a/solution.py
+++ b/solution.py
@@ -9,6 +9,7 @@
 
 LANES = 128
 SCALAR_ROWS = 8
+FLAG = 32.0
 damping = 0.85
 VMEM = pl.BlockSpec(memory_space=pltpu.VMEM)
 HBM = pl.BlockSpec(memory_space=pltpu.HBM)
@@ -37,7 +38,7 @@
 
 
 def prepare(*refs):
-    arguments, (payload, select, keep, dest_ids, tiles), scratch, sems = refs[:7], refs[7:12], refs[12:18], refs[18]
+    arguments, (payload, select, keep, dest_ids, tiles, start), scratch, sems = refs[:7], refs[7:13], refs[13:19], refs[19]
     copies = [
         pltpu.make_async_copy(source, target, sems.at[i])
         for i, (source, target) in enumerate(zip(arguments, (*scratch, tiles), strict=True))
@@ -48,9 +49,15 @@
         copy.wait()
     rank, degree, dangling, dest, src, fill = scratch
     share = rank.shape[0]
-    weight = (1.0 - dangling[...].astype(jnp.float32)) / degree[...].astype(jnp.float32)
-    payload[:, :share] = jnp.broadcast_to(rank[...][None], (payload.shape[0],) + rank.shape)
-    payload[:, share:] = jnp.broadcast_to(weight[None], (payload.shape[0],) + rank.shape)
+    stuck = dangling[...] > 0
+    degree, rank = degree[...].astype(jnp.float32), rank[...]
+    scaled = (rank * (1.0 / degree)).astype(jnp.bfloat16).astype(jnp.float32)
+    high = rank.astype(jnp.bfloat16).astype(jnp.float32)
+    planes = [jnp.where(stuck, high, scaled), jnp.where(stuck, rank - high, degree)]
+    for i, plane in enumerate(planes):
+        rows = slice(i * share, (i + 1) * share)
+        payload[:, rows] = jnp.broadcast_to(plane.astype(jnp.bfloat16)[None], (payload.shape[0], share, LANES))
+    start[...] = rank
     lane = lax.broadcasted_iota(jnp.int32, select.shape, 1).astype(jnp.float32)
     select[...] = jnp.where(column(src[...]) == lane, 1.0, 0.0).astype(jnp.bfloat16)
     lane = lax.broadcasted_iota(jnp.int32, keep.shape, 1).astype(jnp.float32)
@@ -59,17 +66,30 @@
     copies[-1].wait()
 
 
-def products(rank, weight, select, keep, dest_ids, tiles, sources, dest_tiles):
-    scaled = (rank * weight).astype(jnp.bfloat16)
-    picked = jnp.dot(select[...], scaled, preferred_element_type=jnp.float32)
+def unpack(got):
+    blocks, both, _ = got.shape
+    one = got[:, : both // 2].reshape(blocks * both // 2, LANES).astype(jnp.float32)
+    two = got[:, both // 2 :].reshape(blocks * both // 2, LANES).astype(jnp.float32)
+    return one, two, two < FLAG
+
+
+def products(scaled, select, keep, dest_ids, tiles, sources, dest_tiles):
+    picked = jnp.dot(select[...], scaled.astype(jnp.bfloat16), preferred_element_type=jnp.float32)
     sources[...] = jnp.where(keep[...] > 0.0, picked, 0.0)
     target = lax.broadcasted_iota(jnp.int32, (dest_tiles, LANES), 0)
     total = jnp.zeros((dest_tiles, LANES), jnp.float32)
-    for k in range(tiles.shape[0]):
-        placed = jnp.where(dest_ids[pl.ds(k, 1), :] == target, sources[pl.ds(k, 1), :], 0.0)
+    slots = tiles.shape[0]
+    together = 2 - slots % 2
+
+    def placed(k):
+        line = jnp.where(dest_ids[pl.ds(k, 1), :] == target, sources[pl.ds(k, 1), :], 0.0)
+        return line.astype(jnp.bfloat16)
+
+    for first_slot in range(0, slots, together):
+        group = range(first_slot, first_slot + together)
         total += lax.dot_general(
-            placed.astype(jnp.bfloat16),
-            tiles[k],
+            jnp.concatenate([placed(k) for k in group], axis=1),
+            jnp.concatenate([tiles[k] for k in group], axis=1),
             (((1,), (1,)), ((), ())),
             preferred_element_type=jnp.float32,
         )
@@ -79,10 +99,10 @@
 def first(pages, rows, got, select, keep, dest_ids, tiles, send, sources):
     blocks, both, _ = got.shape
     share, half = both // 2, both // 4
-    rank = got[:, :share].reshape(blocks * share, LANES)
-    weight = got[:, share:].reshape(blocks * share, LANES)
-    lost = jnp.sum(jnp.where(weight == 0.0, rank, 0.0))
-    total = products(rank, weight, select, keep, dest_ids, tiles, sources, rows * share) + lost / pages
+    one, two, stuck = unpack(got)
+    lost = jnp.sum(jnp.where(stuck, one + two, 0.0))
+    scaled = jnp.where(stuck, 0.0, one)
+    total = products(scaled, select, keep, dest_ids, tiles, sources, rows * share) + lost / pages
     for b in range(blocks):
         for w in range(rows):
             start = w * share + (b % 2) * half
@@ -98,7 +118,7 @@
         mine[b] = damping * total + (1.0 - damping)
 
 
-def second(pages, rows, mine, other, got, select, keep, dest_ids, tiles, send, own_part, sources):
+def second(pages, rows, mine, other, got, start, select, keep, dest_ids, tiles, send, own_part, sources):
     blocks, both, _ = got.shape
     share, half = both // 2, both // 4
     b, w = lax.axis_index("blk"), lax.axis_index("row")
@@ -106,15 +126,16 @@
     low = jnp.where(core0, mine[...], other[...])
     high = jnp.where(core0, other[...], mine[...])
     rank = jnp.concatenate([low, high], axis=1).reshape(blocks * share, LANES)
-    rank0 = got[:, :share].reshape(blocks * share, LANES)
-    weight = got[:, share:].reshape(blocks * share, LANES)
-    change = jnp.sum(jnp.abs(rank - rank0))
-    lost = jnp.sum(jnp.where(weight == 0.0, rank, 0.0))
-    total = products(rank, weight, select, keep, dest_ids, tiles, sources, rows * share)
+    _, degree, stuck = unpack(got)
+    lost = jnp.sum(jnp.where(stuck, rank, 0.0))
+    scaled = rank * jnp.where(stuck, 0.0, 1.0 / degree)
+    total = products(scaled, select, keep, dest_ids, tiles, sources, rows * share)
     total = damping * (total + lost / pages)
     own_low = jnp.where(core0, mine[b], other[b])
     own_high = jnp.where(core0, other[b], mine[b])
-    own = jnp.concatenate([own_low, own_high], axis=0) - (1.0 - damping)
+    own = jnp.concatenate([own_low, own_high], axis=0)
+    change = jnp.sum(jnp.abs(own - start[...]))
+    own -= 1.0 - damping
     kept = jnp.zeros((share, LANES), jnp.float32)
     for r in range(rows):
         piece = total[r * share : (r + 1) * share]
@@ -134,9 +155,8 @@
     for r in range(1, rows):
         total += got[r]
     change1 = jnp.sum(jnp.abs(total[:dest_tiles]))
-    change0 = jnp.where(lax.axis_index("blk") == 0, total[dest_tiles:, :], 0.0)[:1]
     lane = lax.broadcasted_iota(jnp.int32, (1, LANES), 1)
-    line = jnp.where(lane == 0, change0, change1)
+    line = jnp.where(lane == 0, total[dest_tiles : dest_tiles + 1], change1)
     send[...] = jnp.broadcast_to(line, send.shape)
 
 
@@ -159,14 +179,15 @@
     sources = (pltpu.VMEM((slots, LANES), jnp.float32),)
 
     arguments = (rank_start, out_degree, dangling, tile_dest[None], tile_src[None], tile_fill[None], tiles)
-    payload, *table = call(
+    payload, *table, start = call(
         prepare,
         (
-            f32((blocks, 2 * share, LANES)),
+            jax.ShapeDtypeStruct((blocks, 2 * share, LANES), jnp.bfloat16),
             jax.ShapeDtypeStruct((slots, blocks * share), jnp.bfloat16),
             f32((slots, LANES)),
             jax.ShapeDtypeStruct((slots, LANES), jnp.int32),
             jax.ShapeDtypeStruct(tiles.shape, tiles.dtype),
+            f32((share, LANES)),
         ),
         (*(pltpu.VMEM(a.shape, a.dtype) for a in arguments[:-1]), pltpu.SemaphoreType.DMA((len(arguments),))),
         HBM,
@@ -182,7 +203,7 @@
         functools.partial(second, pages, rows),
         (f32((rows, dest_tiles + SCALAR_ROWS, LANES)), f32((share, LANES))),
         sources,
-    )(mine, other, got_a, *table)
+    )(mine, other, got_a, start, *table)
 
     got_d = lax.all_to_all(send, "row", 0, 0)
     send = call(block_change, f32((blocks, LANES)))(got_d)

time: 45.3 us -> 44.2 us (0.976)
  Pallas kernels: 3.94 us -> 3.36 us
  blocking collectives: 39.1 us -> 38.6 us
    pallas_call x6, Pallas kernels: 3.94 us -> 3.36 us  [run(): pl.pallas_call(kernel, out_shape=outs, in_specs=(space,) * len(arguments)...]
    all_to_all x1, blocking collectives: 10.5 us -> 10 us  [local(): got_a = lax.all_to_all(payload, 'blk', 0, 0)]
where the time goes in v3:
time: 44.2 us; the launch traced here: 43.9 us
  blocking collectives  38.6 us (87%)
  Pallas kernels  3.36 us (8%)
  waiting for transfers between devices  1.19 us (3%)
  between operations  0.66 us (1%)
    all_to_all x1, blocking collectives, local(): got_b = lax.all_to_all(send, ('blk', 'row'), 0, 0)  12.2 us
    all_to_all x1, blocking collectives, local(): got_a = lax.all_to_all(payload, 'blk', 0, 0)  10 us
    all_to_all x1, blocking collectives, local(): got_d = lax.all_to_all(send, 'row', 0, 0)  9.39 us
    all_to_all x1, blocking collectives, local(): got_e = lax.all_to_all(send, 'blk', 0, 0, tiled=True)  7.05 us
    pallas_call x6, Pallas kernels, run(): pl.pallas_call(kernel, out_shape=outs, in_specs=(space,) * len(arguments)...  3.36 us
    ppermute x1, waiting for transfers between devices, local(): other = lax.ppermute(mine, 'blk', [(i, i ^ 1) for i in range(blocks)])  1.19 us
  transfers between devices with their start and end apart: 1, of which 1 were waited for; matrix products, arithmetic and copies ran while one was open for 0% of the time, Pallas kernels for 0%

profile of v3, /device:TPU:0, one launch (start us, length us, event | category | flops | bytes accessed | tf_op | source)
XLA Modules:
  0.0 43.9 jit_solution(14855098161978043568)
XLA Ops:
  0.6 1.4 %shard_map.86 = (bf16[8,32,128]{2,1,0:T(8,128)(2,1)S(1)}, bf16[32,128]{1,0:T(8,128)(2,1)S(1)}, f32[32,128]{1,0:T(8,128)S(1)}, s32[32,128]{1,0:T(8,128)S(1)}, bf1...) custom-call(f32[16,128]{1,0:T(8,128)} %refs_0_.1, s32[16,128]{1,0:T(8,128)} %refs_1_.1, s32[16,128]{1,0:T(8,128)} %refs_2_.1, ...), custom_call_target="tpu_custom_call" | custom-call | flops 1000000 | bytes 1000000 | tf_op jit(solution)/shard_map/pallas_call | solution.py:20
  2.0 10.0 %all_to_all.26.got = bf16[8,32,128]{2,1,0:T(8,128)(2,1)S(1)} all-to-all(bf16[8,32,128]{2,1,0:T(8,128)(2,1)S(1)} %get-tuple-element.10), channel_id=1, replica_groups=mesh['blk'=8,'row'=4] {'blk'}, dimensions={0} | all-to-all | bytes 131072 | tf_op jit(solution)/shard_map/all_to_all | solution.py:196
  12.0 0.6 %shard_map.87 = f32[32,8,128]{2,1,0:T(8,128)S(1)} custom-call(bf16[8,32,128]{2,1,0:T(8,128)(2,1)S(1)} %all_to_all.26.got, bf16[32,128]{1,0:T(8,128)(2,1)S(1)} %get-tuple-element.11.select, f32[32,128]{1,0:T(8,128)S(1)} %get-tuple-element.12.keep, s32[32,128]{1,0:T(8,128)S(1)} %get-tuple-element.13.dest_ids, bf16[32,128,128]{2,1,0:T(8,128)(2,1)S(1)} %get-tuple-element.14.tiles), custom_call_target="tpu_custom_call" | custom-call | flops 1000000 | bytes 1000000 | tf_op jit(solution)/shard_map/pallas_call | solution.py:20
  12.6 12.2 %all_to_all.27.got = f32[32,8,128]{2,1,0:T(8,128)S(1)} all-to-all(f32[32,8,128]{2,1,0:T(8,128)S(1)} %shard_map.87), channel_id=1, replica_groups=mesh['blk'=8,'row'=4] {'blk','row'}, dimensions={0} | all-to-all | bytes 262144 | tf_op jit(solution)/shard_map/all_to_all | solution.py:199
  24.8 0.1 collective-permute-start
  24.9 1.2 %collective-permute-done.other = f32[8,8,128]{2,1,0:T(8,128)S(1)} collective-permute-done((f32[8,8,128]{2,1,0:T(8,128)S(1)}, f32[8,8,128]{2,1,0:T(8,128)S(1)}, u32[]{:S(2)}, u32[]{:S(2)}) %collective-permute-start) | collective-permute-done | bytes 32800 | tf_op jit(solution)/shard_map/ppermute | solution.py:201
  26.1 0.6 %shard_map.89 = (f32[4,72,128]{2,1,0:T(8,128)S(1)}, f32[16,128]{1,0:T(8,128)S(1)}) custom-call(f32[8,8,128]{2,1,0:T(8,128)S(1)} %shard_map.88.mine, f32[8,8,128]{2,1,0:T(8,128)S(1)} %collective-permute-done.other, bf16[8,32,128]{2,1,0:T(8,128)(2,1)S(1)} %all_to_all.26.got, f32[16,128]{1,0:T(8,128)S(1)} %get-tuple-element.15.start, ...), custom_call_target="tpu_custom_call" | custom-call | flops 1000000 | bytes 1000000 | tf_op jit(solution)/shard_map/pallas_call | solution.py:20
  26.7 9.4 %all_to_all.28.got = f32[4,72,128]{2,1,0:T(8,128)S(1)} all-to-all(f32[4,72,128]{2,1,0:T(8,128)S(1)} %get-tuple-element.16), channel_id=1, replica_groups=mesh['blk'=8,'row'=4] {'row'}, dimensions={0} | all-to-all | bytes 294912 | tf_op jit(solution)/shard_map/all_to_all | solution.py:208
  36.1 0.1 shard_map.90
  36.2 7.1 %all_to_all.29 = f32[8,1,128]{2,1,0:T(1,128)S(1)} all-to-all(f32[8,1,128]{2,1,0:T(1,128)S(1)} %bitcast.8), channel_id=1, replica_groups=mesh['blk'=8,'row'=4] {'blk'}, dimensions={0} | all-to-all | bytes 8192 | tf_op jit(solution)/shard_map/all_to_all | solution.py:211
  43.3 0.6 %shard_map.91 = (f32[16,128]{1,0:T(8,128)}, f32[2]{0:T(128)}) custom-call(f32[4,72,128]{2,1,0:T(8,128)S(1)} %all_to_all.28.got, f32[16,128]{1,0:T(8,128)S(1)} %get-tuple-element.17.own_part, f32[8,128]{1,0:T(8,128)S(1)} %bitcast.7), custom_call_target="tpu_custom_call" | custom-call | flops 1000000 | bytes 1000000 | tf_op jit(solution)/shard_map/pallas_call | solution.py:20
  (1 shorter events, 0.0 us)
Async XLA Ops:
  24.8 1.3 %collective-permute-start = (f32[8,8,128]{2,1,0:T(8,128)S(1)}, f32[8,8,128]{2,1,0:T(8,128)S(1)}, u32[]{:S(2)}, u32[]{:S(2)}) collective-permute-start(f32[8,8,128]{2,1,0:T(8,128)S(1)} %shard_map.88.mine), channel_id=1, source_target_pairs={{0,4},{4,0},{8,12},{12,8},{16,20},{20,16},{24,28},{28,24},{1,5},{5... | collective-permute-start | bytes 98312 | tf_op jit(solution)/shard_map/ppermute | solution.py:201

commit v4 on v3

--- a/solution.py
+++ b/solution.py
@@ -15,7 +15,7 @@
 HBM = pl.BlockSpec(memory_space=pltpu.HBM)
 
 
-def call(kernel, outs, scratch=(), space=VMEM):
+def call(kernel, outs, scratch=(), space=VMEM, flops=1000000):
     def run(*arguments):
         return pl.pallas_call(
             kernel,
@@ -24,7 +24,7 @@
             out_specs=(VMEM,) * len(outs) if isinstance(outs, tuple) else VMEM,
             scratch_shapes=scratch,
             compiler_params=pltpu.CompilerParams(vmem_limit_bytes=24 * 1024 * 1024),
-            cost_estimate=pl.CostEstimate(flops=1000000, bytes_accessed=1000000, transcendentals=0),
+            cost_estimate=pl.CostEstimate(flops=flops, bytes_accessed=1000000, transcendentals=0),
         )(*arguments)
 
     return run
@@ -38,14 +38,14 @@
 
 
 def prepare(*refs):
-    arguments, (payload, select, keep, dest_ids, tiles, start), scratch, sems = refs[:7], refs[7:13], refs[13:19], refs[19]
+    arguments, (payload, select, keep, dest_ids, start), scratch, sems = refs[:6], refs[6:11], refs[11:17], refs[17]
     copies = [
         pltpu.make_async_copy(source, target, sems.at[i])
-        for i, (source, target) in enumerate(zip(arguments, (*scratch, tiles), strict=True))
+        for i, (source, target) in enumerate(zip(arguments, scratch, strict=True))
     ]
     for copy in copies:
         copy.start()
-    for copy in copies[:-1]:
+    for copy in copies:
         copy.wait()
     rank, degree, dangling, dest, src, fill = scratch
     share = rank.shape[0]
@@ -63,7 +63,6 @@
     lane = lax.broadcasted_iota(jnp.int32, keep.shape, 1).astype(jnp.float32)
     keep[...] = jnp.where(lane < column(fill[...]), 1.0, 0.0)
     dest_ids[...] = jnp.broadcast_to(column(dest[...]), dest_ids.shape).astype(jnp.int32)
-    copies[-1].wait()
 
 
 def unpack(got):
@@ -178,7 +177,7 @@
     f32 = functools.partial(jax.ShapeDtypeStruct, dtype=jnp.float32)
     sources = (pltpu.VMEM((slots, LANES), jnp.float32),)
 
-    arguments = (rank_start, out_degree, dangling, tile_dest[None], tile_src[None], tile_fill[None], tiles)
+    arguments = (rank_start, out_degree, dangling, tile_dest[None], tile_src[None], tile_fill[None])
     payload, *table, start = call(
         prepare,
         (
@@ -186,13 +185,14 @@
             jax.ShapeDtypeStruct((slots, blocks * share), jnp.bfloat16),
             f32((slots, LANES)),
             jax.ShapeDtypeStruct((slots, LANES), jnp.int32),
-            jax.ShapeDtypeStruct(tiles.shape, tiles.dtype),
             f32((share, LANES)),
         ),
-        (*(pltpu.VMEM(a.shape, a.dtype) for a in arguments[:-1]), pltpu.SemaphoreType.DMA((len(arguments),))),
+        (*(pltpu.VMEM(a.shape, a.dtype) for a in arguments), pltpu.SemaphoreType.DMA((len(arguments),))),
         HBM,
+        flops=1000000000,
     )(*(pltpu.with_memory_space_constraint(a, pltpu.HBM) for a in arguments))
 
+    table = (*table, tiles)
     got_a = lax.all_to_all(payload, "blk", 0, 0)
     send = call(functools.partial(first, pages, rows), f32((blocks * rows, half, LANES)), sources)(got_a, *table)
 

time: 44.2 us -> 43.8 us (level)
  no operation moved by 1% of the time
where the time goes in v4:
time: 43.8 us; the launch traced here: 43.5 us
  blocking collectives  38.6 us (88%)
  Pallas kernels  2.94 us (7%)
  waiting for transfers between devices  1.19 us (3%)
  between operations  0.67 us (2%)
    all_to_all x1, blocking collectives, local(): got_b = lax.all_to_all(send, ('blk', 'row'), 0, 0)  12.2 us
    all_to_all x1, blocking collectives, local(): got_a = lax.all_to_all(payload, 'blk', 0, 0)  10 us
    all_to_all x1, blocking collectives, local(): got_d = lax.all_to_all(send, 'row', 0, 0)  9.39 us
    all_to_all x1, blocking collectives, local(): got_e = lax.all_to_all(send, 'blk', 0, 0, tiled=True)  7.05 us
    pallas_call x6, Pallas kernels, run(): pl.pallas_call(kernel, out_shape=outs, in_specs=(space,) * len(arguments)...  2.94 us
    ppermute x1, waiting for transfers between devices, local(): other = lax.ppermute(mine, 'blk', [(i, i ^ 1) for i in range(blocks)])  1.19 us
  transfers between devices with their start and end apart: 1, of which 1 were waited for; matrix products, arithmetic and copies ran while one was open for 0% of the time, Pallas kernels for 0%

profile of v4, /device:TPU:0, one launch (start us, length us, event | category | flops | bytes accessed | tf_op | source)
XLA Modules:
  0.0 43.5 jit_solution(17292498320642166300)
XLA Ops:
  0.6 0.0 copy-start
  0.6 1.0 %shard_map.86 = (bf16[8,32,128]{2,1,0:T(8,128)(2,1)S(1)}, bf16[32,128]{1,0:T(8,128)(2,1)S(1)}, f32[32,128]{1,0:T(8,128)S(1)}, s32[32,128]{1,0:T(8,128)S(1)}, f32[16,128]{1,0:T(8,128)S(1)}) custom-call(f32[16,128]{1,0:T(8,128)} %refs_0_.1, s32[16,128]{1,0:T(8,128)} %refs_1_.1, s32[16,128]{1,0:T(8,128)} %refs_2_.1, s32[1,32]{1,0:T(1,128)} %bitcast.9, ...), custom_call_target="tpu_custom_call" | custom-call | flops 1000000000 | bytes 1000000 | tf_op jit(solution)/shard_map/pallas_call | solution.py:20
  1.6 10.0 %all_to_all.26.got = bf16[8,32,128]{2,1,0:T(8,128)(2,1)S(1)} all-to-all(bf16[8,32,128]{2,1,0:T(8,128)(2,1)S(1)} %get-tuple-element.9), channel_id=1, replica_groups=mesh['blk'=8,'row'=4] {'blk'}, dimensions={0} | all-to-all | bytes 131072 | tf_op jit(solution)/shard_map/all_to_all | solution.py:196
  11.6 0.0 copy-done
  11.6 0.6 %shard_map.87 = f32[32,8,128]{2,1,0:T(8,128)S(1)} custom-call(bf16[8,32,128]{2,1,0:T(8,128)(2,1)S(1)} %all_to_all.26.got, bf16[32,128]{1,0:T(8,128)(2,1)S(1)} %get-tuple-element.10.select, f32[32,128]{1,0:T(8,128)S(1)} %get-tuple-element.11.keep, s32[32,128]{1,0:T(8,128)S(1)} %get-tuple-element.12.dest_ids, bf16[32,128,128]{2,1,0:T(8,128)(2,1)S(1)} %copy-done), custom_call_target="tpu_custom_call" | custom-call | flops 1000000 | bytes 1000000 | tf_op jit(solution)/shard_map/pallas_call | solution.py:20
  12.2 12.2 %all_to_all.27.got = f32[32,8,128]{2,1,0:T(8,128)S(1)} all-to-all(f32[32,8,128]{2,1,0:T(8,128)S(1)} %shard_map.87), channel_id=1, replica_groups=mesh['blk'=8,'row'=4] {'blk','row'}, dimensions={0} | all-to-all | bytes 262144 | tf_op jit(solution)/shard_map/all_to_all | solution.py:199
  24.4 0.1 collective-permute-start
  24.5 1.2 %collective-permute-done.other = f32[8,8,128]{2,1,0:T(8,128)S(1)} collective-permute-done((f32[8,8,128]{2,1,0:T(8,128)S(1)}, f32[8,8,128]{2,1,0:T(8,128)S(1)}, u32[]{:S(2)}, u32[]{:S(2)}) %collective-permute-start) | collective-permute-done | bytes 32800 | tf_op jit(solution)/shard_map/ppermute | solution.py:201
  25.7 0.6 %shard_map.89 = (f32[4,72,128]{2,1,0:T(8,128)S(1)}, f32[16,128]{1,0:T(8,128)S(1)}) custom-call(f32[8,8,128]{2,1,0:T(8,128)S(1)} %shard_map.88.mine, f32[8,8,128]{2,1,0:T(8,128)S(1)} %collective-permute-done.other, bf16[8,32,128]{2,1,0:T(8,128)(2,1)S(1)} %all_to_all.26.got, f32[16,128]{1,0:T(8,128)S(1)} %get-tuple-element.13.start, ...), custom_call_target="tpu_custom_call" | custom-call | flops 1000000 | bytes 1000000 | tf_op jit(solution)/shard_map/pallas_call | solution.py:20
  26.3 9.4 %all_to_all.28.got = f32[4,72,128]{2,1,0:T(8,128)S(1)} all-to-all(f32[4,72,128]{2,1,0:T(8,128)S(1)} %get-tuple-element.14), channel_id=1, replica_groups=mesh['blk'=8,'row'=4] {'row'}, dimensions={0} | all-to-all | bytes 294912 | tf_op jit(solution)/shard_map/all_to_all | solution.py:208
  35.7 0.1 shard_map.90
  35.8 7.1 %all_to_all.29 = f32[8,1,128]{2,1,0:T(1,128)S(1)} all-to-all(f32[8,1,128]{2,1,0:T(1,128)S(1)} %bitcast.8), channel_id=1, replica_groups=mesh['blk'=8,'row'=4] {'blk'}, dimensions={0} | all-to-all | bytes 8192 | tf_op jit(solution)/shard_map/all_to_all | solution.py:211
  42.9 0.6 %shard_map.91 = (f32[16,128]{1,0:T(8,128)}, f32[2]{0:T(128)}) custom-call(f32[4,72,128]{2,1,0:T(8,128)S(1)} %all_to_all.28.got, f32[16,128]{1,0:T(8,128)S(1)} %get-tuple-element.15.own_part, f32[8,128]{1,0:T(8,128)S(1)} %bitcast.7), custom_call_target="tpu_custom_call" | custom-call | flops 1000000 | bytes 1000000 | tf_op jit(solution)/shard_map/pallas_call | solution.py:20
  (1 shorter events, 0.0 us)
Async XLA Ops:
  0.6 11.0 %copy-start = (bf16[32,128,128]{2,1,0:T(8,128)(2,1)S(1)}, bf16[32,128,128]{2,1,0:T(8,128)(2,1)}, u32[]{:S(2)}) copy-start(bf16[32,128,128]{2,1,0:T(8,128)(2,1)} %tiles.3) | copy-start | bytes 3145732
  24.4 1.3 %collective-permute-start = (f32[8,8,128]{2,1,0:T(8,128)S(1)}, f32[8,8,128]{2,1,0:T(8,128)S(1)}, u32[]{:S(2)}, u32[]{:S(2)}) collective-permute-start(f32[8,8,128]{2,1,0:T(8,128)S(1)} %shard_map.88.mine), channel_id=1, source_target_pairs={{0,4},{4,0},{8,12},{12,8},{16,20},{20,16},{24,28},{28,24},{1,5},{5... | collective-permute-start | bytes 98312 | tf_op jit(solution)/shard_map/ppermute | solution.py:201

commit v5 on v4

--- a/solution.py
+++ b/solution.py
@@ -65,10 +65,11 @@
     dest_ids[...] = jnp.broadcast_to(column(dest[...]), dest_ids.shape).astype(jnp.int32)
 
 
-def unpack(got):
-    blocks, both, _ = got.shape
-    one = got[:, : both // 2].reshape(blocks * both // 2, LANES).astype(jnp.float32)
-    two = got[:, both // 2 :].reshape(blocks * both // 2, LANES).astype(jnp.float32)
+def unpack(got, order):
+    share = got.shape[1] // 2
+    place = [order.index(b) for b in range(len(order))]
+    one = jnp.concatenate([got[p, :share] for p in place], axis=0).astype(jnp.float32)
+    two = jnp.concatenate([got[p, share:] for p in place], axis=0).astype(jnp.float32)
     return one, two, two < FLAG
 
 
@@ -95,44 +96,39 @@
     return total
 
 
-def first(pages, rows, got, select, keep, dest_ids, tiles, send, sources):
-    blocks, both, _ = got.shape
-    share, half = both // 2, both // 4
-    one, two, stuck = unpack(got)
+def first(pages, rows, order, members, got, select, keep, dest_ids, tiles, send, sources):
+    share = got.shape[1] // 2
+    one, two, stuck = unpack(got, order)
     lost = jnp.sum(jnp.where(stuck, one + two, 0.0))
     scaled = jnp.where(stuck, 0.0, one)
     total = products(scaled, select, keep, dest_ids, tiles, sources, rows * share) + lost / pages
-    for b in range(blocks):
-        for w in range(rows):
-            start = w * share + (b % 2) * half
-            send[b * rows + w] = total[start : start + half]
-
-
-def gather_rows(rows, got, mine):
-    blocks = mine.shape[0]
-    for b in range(blocks):
-        total = got[b * rows]
+    for i, (_, w) in enumerate(members):
+        send[i] = total[w * share : (w + 1) * share]
+
+
+def gather_rows(rows, members, got, mine):
+    for pair in range(mine.shape[0]):
+        total = got[members.index((pair, 0))]
         for w in range(1, rows):
-            total += got[b * rows + w]
-        mine[b] = damping * total + (1.0 - damping)
-
-
-def second(pages, rows, mine, other, got, start, select, keep, dest_ids, tiles, send, own_part, sources):
-    blocks, both, _ = got.shape
-    share, half = both // 2, both // 4
+            total += got[members.index((pair, w))]
+        mine[pair] = damping * total + (1.0 - damping)
+
+
+def second(pages, rows, order, mine, other, got, start, select, keep, dest_ids, tiles, send, own_part, sources):
+    share = got.shape[1] // 2
     b, w = lax.axis_index("blk"), lax.axis_index("row")
     core0 = lax.rem(b, 2) == 0
-    low = jnp.where(core0, mine[...], other[...])
-    high = jnp.where(core0, other[...], mine[...])
-    rank = jnp.concatenate([low, high], axis=1).reshape(blocks * share, LANES)
-    _, degree, stuck = unpack(got)
+    pieces = []
+    for pair in range(mine.shape[0]):
+        pieces.append(jnp.where(core0, mine[pair], other[pair]))
+        pieces.append(jnp.where(core0, other[pair], mine[pair]))
+    rank = jnp.concatenate(pieces, axis=0)
+    _, degree, stuck = unpack(got, order)
     lost = jnp.sum(jnp.where(stuck, rank, 0.0))
     scaled = rank * jnp.where(stuck, 0.0, 1.0 / degree)
     total = products(scaled, select, keep, dest_ids, tiles, sources, rows * share)
     total = damping * (total + lost / pages)
-    own_low = jnp.where(core0, mine[b], other[b])
-    own_high = jnp.where(core0, other[b], mine[b])
-    own = jnp.concatenate([own_low, own_high], axis=0)
+    own = mine[lax.div(b, 2)]
     change = jnp.sum(jnp.abs(own - start[...]))
     own -= 1.0 - damping
     kept = jnp.zeros((share, LANES), jnp.float32)
@@ -159,12 +155,12 @@
     send[...] = jnp.broadcast_to(line, send.shape)
 
 
-def finish(rows, got, own_part, changes, rank, out):
+def finish(order, got, own_part, changes, rank, out):
     share = rank.shape[0]
     w = lax.axis_index("row")
     total = own_part[...] + (1.0 - damping)
-    for r in range(rows):
-        total += jnp.where(w == r, 0.0, got[r, pl.ds(w * share, share), :])
+    for i, r in enumerate(order):
+        total += jnp.where(w == r, 0.0, got[i, pl.ds(w * share, share), :])
     rank[...] = total
     out[...] = jnp.sum(changes[...], axis=0)[: out.shape[0]]
 
@@ -172,7 +168,10 @@
 def local(rank_start, tiles, tile_dest, tile_src, tile_fill, out_degree, dangling):
     share, slots = rank_start.shape[0], tiles.shape[0]
     blocks, rows = lax.axis_size("blk"), lax.axis_size("row")
-    half, dest_tiles = share // 2, rows * share
+    dest_tiles = rows * share
+    by_block = list(range(blocks))[::-1]
+    by_row = [rows // 2] + [w for w in range(rows) if w != rows // 2]
+    members = [(pair, w) for w in by_row for pair in range(blocks // 2)[::-1]]
     pages = float(blocks * rows * share * LANES)
     f32 = functools.partial(jax.ShapeDtypeStruct, dtype=jnp.float32)
     sources = (pltpu.VMEM((slots, LANES), jnp.float32),)
@@ -192,24 +191,27 @@
         flops=1000000000,
     )(*(pltpu.with_memory_space_constraint(a, pltpu.HBM) for a in arguments))
 
+    got_a = lax.all_to_all(payload, "blk", 0, 0, axis_index_groups=[by_block])
     table = (*table, tiles)
-    got_a = lax.all_to_all(payload, "blk", 0, 0)
-    send = call(functools.partial(first, pages, rows), f32((blocks * rows, half, LANES)), sources)(got_a, *table)
-
-    got_b = lax.all_to_all(send, ("blk", "row"), 0, 0)
-    mine = call(functools.partial(gather_rows, rows), f32((blocks, half, LANES)))(got_b)
+    send = call(functools.partial(first, pages, rows, by_block, members), f32((len(members), share, LANES)), sources)(
+        got_a, *table
+    )
+
+    groups = [[(2 * pair + core) * rows + w for pair, w in members] for core in range(2)]
+    got_b = lax.all_to_all(send, ("blk", "row"), 0, 0, axis_index_groups=groups)
+    mine = call(functools.partial(gather_rows, rows, members), f32((blocks // 2, share, LANES)))(got_b)
     other = lax.ppermute(mine, "blk", [(i, i ^ 1) for i in range(blocks)])
     send, own_part = call(
-        functools.partial(second, pages, rows),
+        functools.partial(second, pages, rows, by_block),
         (f32((rows, dest_tiles + SCALAR_ROWS, LANES)), f32((share, LANES))),
         sources,
     )(mine, other, got_a, start, *table)
 
-    got_d = lax.all_to_all(send, "row", 0, 0)
+    got_d = lax.all_to_all(send, "row", 0, 0, axis_index_groups=[by_row])
     send = call(block_change, f32((blocks, LANES)))(got_d)
 
-    got_e = lax.all_to_all(send, "blk", 0, 0, tiled=True)
-    return call(functools.partial(finish, rows), (f32((share, LANES)), f32((2,))))(got_d, own_part, got_e)
+    got_e = lax.all_to_all(send, "blk", 0, 0, tiled=True, axis_index_groups=[by_block])
+    return call(functools.partial(finish, by_row), (f32((share, LANES)), f32((2,))))(got_d, own_part, got_e)
 
 
 def solution(mesh):

time: 43.8 us -> 39.7 us (0.906)
  blocking collectives: 38.6 us -> 34.6 us
    all_to_all x4, blocking collectives: 38.6 us -> 34.6 us  [the longest x1 11.1 us: local(): got_b = lax.all_to_all(send, ('blk', 'row'), 0, 0, axis_index_groups=groups)]
where the time goes in v5:
time: 39.7 us; the launch traced here: 39.5 us
  blocking collectives  34.6 us (87%)
  Pallas kernels  2.94 us (7%)
  waiting for transfers between devices  1.19 us (3%)
  between operations  0.67 us (2%)
    all_to_all x1, blocking collectives, local(): got_b = lax.all_to_all(send, ('blk', 'row'), 0, 0, axis_index_groups=groups)  11.1 us
    all_to_all x1, blocking collectives, local(): got_d = lax.all_to_all(send, 'row', 0, 0, axis_index_groups=[by_row])  8.84 us
    all_to_all x1, blocking collectives, local(): got_a = lax.all_to_all(payload, 'blk', 0, 0, axis_index_groups=[by_block])  8.39 us
    all_to_all x1, blocking collectives, local(): lax.all_to_all(send, 'blk', 0, 0, tiled=True, axis_index_groups=[by_block])  6.22 us
    pallas_call x6, Pallas kernels, run(): pl.pallas_call(kernel, out_shape=outs, in_specs=(space,) * len(arguments)...  2.94 us
    ppermute x1, waiting for transfers between devices, local(): other = lax.ppermute(mine, 'blk', [(i, i ^ 1) for i in range(blocks)])  1.19 us
  transfers between devices with their start and end apart: 1, of which 1 were waited for; matrix products, arithmetic and copies ran while one was open for 0% of the time, Pallas kernels for 0%

profile of v5, /device:TPU:0, one launch (start us, length us, event | category | flops | bytes accessed | tf_op | source)
XLA Modules:
  0.0 39.5 jit_solution(35201945356194837)
XLA Ops:
  0.6 0.0 copy-start
  0.6 1.0 %shard_map.86 = (bf16[8,32,128]{2,1,0:T(8,128)(2,1)S(1)}, bf16[32,128]{1,0:T(8,128)(2,1)S(1)}, f32[32,128]{1,0:T(8,128)S(1)}, s32[32,128]{1,0:T(8,128)S(1)}, f32[16,128]{1,0:T(8,128)S(1)}) custom-call(f32[16,128]{1,0:T(8,128)} %refs_0_.1, s32[16,128]{1,0:T(8,128)} %refs_1_.1, s32[16,128]{1,0:T(8,128)} %refs_2_.1, s32[1,32]{1,0:T(1,128)} %bitcast.9, ...), custom_call_target="tpu_custom_call" | custom-call | flops 1000000000 | bytes 1000000 | tf_op jit(solution)/shard_map/pallas_call | solution.py:20
  1.6 8.4 %all_to_all.26.got = bf16[8,32,128]{2,1,0:T(8,128)(2,1)S(1)} all-to-all(bf16[8,32,128]{2,1,0:T(8,128)(2,1)S(1)} %get-tuple-element.9), channel_id=1, replica_groups={{28,24,20,16,12,8,4,0},{29,25,21,17,13,9,5,1},{30,26,22,18,14,10,6,2},{..., dimensions={0} | all-to-all | bytes 131072 | tf_op jit(solution)/shard_map/all_to_all | solution.py:194
  10.0 0.0 copy-done
  10.0 0.6 %shard_map.87 = f32[16,16,128]{2,1,0:T(8,128)S(1)} custom-call(bf16[8,32,128]{2,1,0:T(8,128)(2,1)S(1)} %all_to_all.26.got, bf16[32,128]{1,0:T(8,128)(2,1)S(1)} %get-tuple-element.10.select, f32[32,128]{1,0:T(8,128)S(1)} %get-tuple-element.11.keep, s32[32,128]{1,0:T(8,128)S(1)} %get-tuple-element.12.dest_ids, bf16[32,128,128]{2,1,0:T(8,128)(2,1)S(1)} %copy-done), custom_call_target="tpu_custom_call" | custom-call | flops 1000000 | bytes 1000000 | tf_op jit(solution)/shard_map/pallas_call | solution.py:20
  10.6 11.1 %all_to_all.27.got = f32[16,16,128]{2,1,0:T(8,128)S(1)} all-to-all(f32[16,16,128]{2,1,0:T(8,128)S(1)} %shard_map.87), channel_id=1, replica_groups={{26,18,10,2,24,16,8,0,25,17,9,1,27,19,11,3},{30,22,14,6,28,20,12,4,29,2..., dimensions={0} | all-to-all | bytes 262144 | tf_op jit(solution)/shard_map/all_to_all | solution.py:201
  21.8 0.1 collective-permute-start
  21.8 1.2 %collective-permute-done.other = f32[4,16,128]{2,1,0:T(8,128)S(1)} collective-permute-done((f32[4,16,128]{2,1,0:T(8,128)S(1)}, f32[4,16,128]{2,1,0:T(8,128)S(1)}, u32[]{:S(2)}, u32[]{:S(2)}) %collective-permute-start) | collective-permute-done | bytes 32800 | tf_op jit(solution)/shard_map/ppermute | solution.py:203
  23.0 0.6 %shard_map.89 = (f32[4,72,128]{2,1,0:T(8,128)S(1)}, f32[16,128]{1,0:T(8,128)S(1)}) custom-call(f32[4,16,128]{2,1,0:T(8,128)S(1)} %shard_map.88.mine, f32[4,16,128]{2,1,0:T(8,128)S(1)} %collective-permute-done.other, bf16[8,32,128]{2,1,0:T(8,128)(2,1)S(1)} %all_to_all.26.got, f32[16,128]{1,0:T(8,128)S(1)} %get-tuple-element.13.start, ...), custom_call_target="tpu_custom_call" | custom-call | flops 1000000 | bytes 1000000 | tf_op jit(solution)/shard_map/pallas_call | solution.py:20
  23.7 8.8 %all_to_all.28.got = f32[4,72,128]{2,1,0:T(8,128)S(1)} all-to-all(f32[4,72,128]{2,1,0:T(8,128)S(1)} %get-tuple-element.14), channel_id=1, replica_groups={{2,0,1,3},{6,4,5,7},{10,8,9,11},{14,12,13,15},{18,16,17,19},{22,20,21,2..., dimensions={0} | all-to-all | bytes 294912 | tf_op jit(solution)/shard_map/all_to_all | solution.py:210
  32.5 0.1 shard_map.90
  32.6 6.2 %all_to_all.29 = f32[8,1,128]{2,1,0:T(1,128)S(1)} all-to-all(f32[8,1,128]{2,1,0:T(1,128)S(1)} %bitcast.8), channel_id=1, replica_groups={{28,24,20,16,12,8,4,0},{29,25,21,17,13,9,5,1},{30,26,22,18,14,10,6,2},{..., dimensions={0} | all-to-all | bytes 8192 | tf_op jit(solution)/shard_map/all_to_all | solution.py:213
  38.9 0.6 %shard_map.91 = (f32[16,128]{1,0:T(8,128)}, f32[2]{0:T(128)}) custom-call(f32[4,72,128]{2,1,0:T(8,128)S(1)} %all_to_all.28.got, f32[16,128]{1,0:T(8,128)S(1)} %get-tuple-element.15.own_part, f32[8,128]{1,0:T(8,128)S(1)} %bitcast.7), custom_call_target="tpu_custom_call" | custom-call | flops 1000000 | bytes 1000000 | tf_op jit(solution)/shard_map/pallas_call | solution.py:20
  (1 shorter events, 0.0 us)
Async XLA Ops:
  0.6 9.4 %copy-start = (bf16[32,128,128]{2,1,0:T(8,128)(2,1)S(1)}, bf16[32,128,128]{2,1,0:T(8,128)(2,1)}, u32[]{:S(2)}) copy-start(bf16[32,128,128]{2,1,0:T(8,128)(2,1)} %tiles.3) | copy-start | bytes 3145732
  21.8 1.3 %collective-permute-start = (f32[4,16,128]{2,1,0:T(8,128)S(1)}, f32[4,16,128]{2,1,0:T(8,128)S(1)}, u32[]{:S(2)}, u32[]{:S(2)}) collective-permute-start(f32[4,16,128]{2,1,0:T(8,128)S(1)} %shard_map.88.mine), channel_id=1, source_target_pairs={{0,4},{4,0},{8,12},{12,8},{16,20},{20,16},{24,28},{28,24},{1,5},{5... | collective-permute-start | bytes 98312 | tf_op jit(solution)/shard_map/ppermute | solution.py:203

commit v6 on v5

--- a/solution.py
+++ b/solution.py
@@ -73,7 +73,7 @@
     return one, two, two < FLAG
 
 
-def products(scaled, select, keep, dest_ids, tiles, sources, dest_tiles):
+def products(scaled, select, keep, dest_ids, tiles, sources, dest_tiles, turned=False):
     picked = jnp.dot(select[...], scaled.astype(jnp.bfloat16), preferred_element_type=jnp.float32)
     sources[...] = jnp.where(keep[...] > 0.0, picked, 0.0)
     target = lax.broadcasted_iota(jnp.int32, (dest_tiles, LANES), 0)
@@ -89,8 +89,8 @@
         group = range(first_slot, first_slot + together)
         total += lax.dot_general(
             jnp.concatenate([placed(k) for k in group], axis=1),
-            jnp.concatenate([tiles[k] for k in group], axis=1),
-            (((1,), (1,)), ((), ())),
+            jnp.concatenate([tiles[k] for k in group], axis=0 if turned else 1),
+            (((1,), (0 if turned else 1,)), ((), ())),
             preferred_element_type=jnp.float32,
         )
     return total
@@ -102,33 +102,51 @@
     lost = jnp.sum(jnp.where(stuck, one + two, 0.0))
     scaled = jnp.where(stuck, 0.0, one)
     total = products(scaled, select, keep, dest_ids, tiles, sources, rows * share) + lost / pages
-    for i, (_, w) in enumerate(members):
+    for i, w in enumerate(members):
         send[i] = total[w * share : (w + 1) * share]
 
 
-def gather_rows(rows, members, got, mine):
-    for pair in range(mine.shape[0]):
-        total = got[members.index((pair, 0))]
-        for w in range(1, rows):
-            total += got[members.index((pair, w))]
-        mine[pair] = damping * total + (1.0 - damping)
-
-
-def second(pages, rows, order, mine, other, got, start, select, keep, dest_ids, tiles, send, own_part, sources):
-    share = got.shape[1] // 2
+def gather_rows(rows, got, mine):
+    slots = mine.shape[0]
+    for i in range(slots):
+        total = got[i]
+        for r in range(1, rows):
+            total += got[r * slots + i]
+        mine[i] = damping * total + (1.0 - damping)
+
+
+def block_class(b, pairs):
+    return jnp.where(lax.div(b, 2) >= pairs // 2, 1 - lax.rem(b, 2), lax.rem(b, 2))
+
+
+def slot_of(pair, kind, pairs):
+    return (pair + (1 - kind) * (pairs // 2)) % pairs
+
+
+def meanwhile(order, got, tiles, weight, flag, turned):
+    _, degree, stuck = unpack(got, order)
+    weight[...] = jnp.where(stuck, 0.0, 1.0 / degree)
+    flag[...] = jnp.where(stuck, 1.0, 0.0)
+    for k in range(tiles.shape[0]):
+        turned[k] = tiles[k].T
+
+
+def second(pages, rows, mine, other, weight, flag, start, select, keep, dest_ids, tiles, send, own_part, sources):
+    share = mine.shape[1]
     b, w = lax.axis_index("blk"), lax.axis_index("row")
-    core0 = lax.rem(b, 2) == 0
+    pairs = mine.shape[0]
+    kind = block_class(b, pairs)
     pieces = []
-    for pair in range(mine.shape[0]):
-        pieces.append(jnp.where(core0, mine[pair], other[pair]))
-        pieces.append(jnp.where(core0, other[pair], mine[pair]))
+    for block in range(2 * pairs):
+        its = 1 - block % 2 if block // 2 >= pairs // 2 else block % 2
+        slot = slot_of(block // 2, its, pairs)
+        pieces.append(jnp.where(kind == its, mine[slot], other[slot]))
     rank = jnp.concatenate(pieces, axis=0)
-    _, degree, stuck = unpack(got, order)
-    lost = jnp.sum(jnp.where(stuck, rank, 0.0))
-    scaled = rank * jnp.where(stuck, 0.0, 1.0 / degree)
-    total = products(scaled, select, keep, dest_ids, tiles, sources, rows * share)
+    lost = jnp.sum(rank * flag[...])
+    scaled = rank * weight[...]
+    total = products(scaled, select, keep, dest_ids, tiles, sources, rows * share, turned=True)
     total = damping * (total + lost / pages)
-    own = mine[lax.div(b, 2)]
+    own = mine[lax.rem(lax.div(b, 2) + (1 - kind) * (pairs // 2), pairs)]
     change = jnp.sum(jnp.abs(own - start[...]))
     own -= 1.0 - damping
     kept = jnp.zeros((share, LANES), jnp.float32)
@@ -171,7 +189,7 @@
     dest_tiles = rows * share
     by_block = list(range(blocks))[::-1]
     by_row = [rows // 2] + [w for w in range(rows) if w != rows // 2]
-    members = [(pair, w) for w in by_row for pair in range(blocks // 2)[::-1]]
+    members = [w for w in by_row for _ in range(blocks // 2)]
     pages = float(blocks * rows * share * LANES)
     f32 = functools.partial(jax.ShapeDtypeStruct, dtype=jnp.float32)
     sources = (pltpu.VMEM((slots, LANES), jnp.float32),)
@@ -197,15 +215,24 @@
         got_a, *table
     )
 
-    groups = [[(2 * pair + core) * rows + w for pair, w in members] for core in range(2)]
+    pairs = blocks // 2
+    groups = [[None] * (pairs * rows) for _ in range(2)]
+    for b in range(blocks):
+        kind = 1 - b % 2 if b // 2 >= pairs // 2 else b % 2
+        for i, w in enumerate(by_row):
+            groups[kind][i * pairs + slot_of(b // 2, kind, pairs)] = b * rows + w
     got_b = lax.all_to_all(send, ("blk", "row"), 0, 0, axis_index_groups=groups)
-    mine = call(functools.partial(gather_rows, rows, members), f32((blocks // 2, share, LANES)))(got_b)
+    mine = call(functools.partial(gather_rows, rows), f32((pairs, share, LANES)))(got_b)
     other = lax.ppermute(mine, "blk", [(i, i ^ 1) for i in range(blocks)])
+    weight, flag, turned = call(
+        functools.partial(meanwhile, by_block),
+        (f32((blocks * share, LANES)), f32((blocks * share, LANES)), jax.ShapeDtypeStruct(tiles.shape, tiles.dtype)),
+    )(got_a, tiles)
     send, own_part = call(
-        functools.partial(second, pages, rows, by_block),
+        functools.partial(second, pages, rows),
         (f32((rows, dest_tiles + SCALAR_ROWS, LANES)), f32((share, LANES))),
         sources,
-    )(mine, other, got_a, start, *table)
+    )(mine, other, weight, flag, start, *table[:3], turned)
 
     got_d = lax.all_to_all(send, "row", 0, 0, axis_index_groups=[by_row])
     send = call(block_change, f32((blocks, LANES)))(got_d)

time: 39.7 us -> 40.2 us (1.013)
  blocking collectives: 34.6 us -> 35.2 us
  waiting for transfers between devices: 1.19 us -> 0.73 us
    all_to_all x1, blocking collectives: 11.1 us -> 12 us  [local(): got_b = lax.all_to_all(send, ('blk', 'row'), 0, 0, axis_index_groups=groups)]
    ppermute x1, waiting for transfers between devices: 1.19 us -> 0.73 us  [local(): other = lax.ppermute(mine, 'blk', [(i, i ^ 1) for i in range(blocks)])]
    pallas_call x6 -> x7, Pallas kernels: 2.94 us -> 3.1 us  [run(): pl.pallas_call(kernel, out_shape=outs, in_specs=(space,) * len(arguments)...]
  transfers between devices with their start and end apart: 1 -> 1, of which waited for: 1 -> 1; matrix products, arithmetic and copies ran while one was open for 0% -> 0% of each run, Pallas kernels for 0% -> 1%
where the time goes in v6:
time: 40.2 us; the launch traced here: 39.9 us
  blocking collectives  35.2 us (88%)
  Pallas kernels  3.1 us (8%)
  waiting for transfers between devices  0.73 us (2%)
  between operations  0.67 us (2%)
    all_to_all x1, blocking collectives, local(): got_b = lax.all_to_all(send, ('blk', 'row'), 0, 0, axis_index_groups=groups)  12 us
    all_to_all x1, blocking collectives, local(): got_d = lax.all_to_all(send, 'row', 0, 0, axis_index_groups=[by_row])  8.75 us
    all_to_all x1, blocking collectives, local(): got_a = lax.all_to_all(payload, 'blk', 0, 0, axis_index_groups=[by_block])  8.39 us
    all_to_all x1, blocking collectives, local(): lax.all_to_all(send, 'blk', 0, 0, tiled=True, axis_index_groups=[by_block])  6.04 us
    pallas_call x7, Pallas kernels, run(): pl.pallas_call(kernel, out_shape=outs, in_specs=(space,) * len(arguments)...  3.1 us
  transfers between devices with their start and end apart: 1, of which 1 were waited for; matrix products, arithmetic and copies ran while one was open for 0% of the time, Pallas kernels for 1%

profile of v6, /device:TPU:0, one launch (start us, length us, event | category | flops | bytes accessed | tf_op | source)
XLA Modules:
  0.0 39.9 jit_solution(13499903974139701225)
XLA Ops:
  0.6 0.0 copy-start
  0.6 1.0 %shard_map.86 = (bf16[8,32,128]{2,1,0:T(8,128)(2,1)S(1)}, bf16[32,128]{1,0:T(8,128)(2,1)S(1)}, f32[32,128]{1,0:T(8,128)S(1)}, s32[32,128]{1,0:T(8,128)S(1)}, f32[16,128]{1,0:T(8,128)S(1)}) custom-call(f32[16,128]{1,0:T(8,128)} %refs_0_.1, s32[16,128]{1,0:T(8,128)} %refs_1_.1, s32[16,128]{1,0:T(8,128)} %refs_2_.1, s32[1,32]{1,0:T(1,128)} %bitcast.9, ...), custom_call_target="tpu_custom_call" | custom-call | flops 1000000000 | bytes 1000000 | tf_op jit(solution)/shard_map/pallas_call | solution.py:20
  1.6 8.4 %all_to_all.26.got = bf16[8,32,128]{2,1,0:T(8,128)(2,1)S(1)} all-to-all(bf16[8,32,128]{2,1,0:T(8,128)(2,1)S(1)} %get-tuple-element.12), channel_id=1, replica_groups={{28,24,20,16,12,8,4,0},{29,25,21,17,13,9,5,1},{30,26,22,18,14,10,6,2},{..., dimensions={0} | all-to-all | bytes 131072 | tf_op jit(solution)/shard_map/all_to_all | solution.py:212
  10.0 0.0 copy-done
  10.0 0.6 %shard_map.87 = f32[16,16,128]{2,1,0:T(8,128)S(1)} custom-call(bf16[8,32,128]{2,1,0:T(8,128)(2,1)S(1)} %all_to_all.26.got, bf16[32,128]{1,0:T(8,128)(2,1)S(1)} %get-tuple-element.13.select, f32[32,128]{1,0:T(8,128)S(1)} %get-tuple-element.14.keep, s32[32,128]{1,0:T(8,128)S(1)} %get-tuple-element.15.dest_ids, bf16[32,128,128]{2,1,0:T(8,128)(2,1)S(1)} %copy-done), custom_call_target="tpu_custom_call" | custom-call | flops 1000000 | bytes 1000000 | tf_op jit(solution)/shard_map/pallas_call | solution.py:20
  10.6 12.0 %all_to_all.27.got = f32[16,16,128]{2,1,0:T(8,128)S(1)} all-to-all(f32[16,16,128]{2,1,0:T(8,128)S(1)} %shard_map.87), channel_id=1, replica_groups={{22,30,2,10,20,28,0,8,21,29,1,9,23,31,3,11},{6,14,18,26,4,12,16,24,5,13..., dimensions={0} | all-to-all | bytes 262144 | tf_op jit(solution)/shard_map/all_to_all | solution.py:224
  22.6 0.2 collective-permute-start
  22.8 0.3 shard_map.89
  23.1 0.7 %collective-permute-done.other = f32[4,16,128]{2,1,0:T(8,128)S(1)} collective-permute-done((f32[4,16,128]{2,1,0:T(8,128)S(1)}, f32[4,16,128]{2,1,0:T(8,128)S(1)}, u32[]{:S(2)}, u32[]{:S(2)}) %collective-permute-start) | collective-permute-done | bytes 32800 | tf_op jit(solution)/shard_map/ppermute | solution.py:226
  23.9 0.5 %shard_map.90 = (f32[4,72,128]{2,1,0:T(8,128)S(1)}, f32[16,128]{1,0:T(8,128)S(1)}) custom-call(f32[4,16,128]{2,1,0:T(8,128)S(1)} %shard_map.88.mine, f32[4,16,128]{2,1,0:T(8,128)S(1)} %collective-permute-done.other, f32[128,128]{1,0:T(8,128)S(1)} %get-tuple-element.16.weight, f32[128,128]{1,0:T(8,128)S(1)} %get-tuple-element.17.flag, ...), custom_call_target="tpu_custom_call" | custom-call | flops 1000000 | bytes 1000000 | tf_op jit(solution)/shard_map/pallas_call | solution.py:20
  24.3 8.8 %all_to_all.28.got = f32[4,72,128]{2,1,0:T(8,128)S(1)} all-to-all(f32[4,72,128]{2,1,0:T(8,128)S(1)} %get-tuple-element.20), channel_id=1, replica_groups={{2,0,1,3},{6,4,5,7},{10,8,9,11},{14,12,13,15},{18,16,17,19},{22,20,21,2..., dimensions={0} | all-to-all | bytes 294912 | tf_op jit(solution)/shard_map/all_to_all | solution.py:237
  33.1 0.1 shard_map.91
  33.2 6.0 %all_to_all.29 = f32[8,1,128]{2,1,0:T(1,128)S(1)} all-to-all(f32[8,1,128]{2,1,0:T(1,128)S(1)} %bitcast.8), channel_id=1, replica_groups={{28,24,20,16,12,8,4,0},{29,25,21,17,13,9,5,1},{30,26,22,18,14,10,6,2},{..., dimensions={0} | all-to-all | bytes 8192 | tf_op jit(solution)/shard_map/all_to_all | solution.py:240
  39.3 0.6 %shard_map.92 = (f32[16,128]{1,0:T(8,128)}, f32[2]{0:T(128)}) custom-call(f32[4,72,128]{2,1,0:T(8,128)S(1)} %all_to_all.28.got, f32[16,128]{1,0:T(8,128)S(1)} %get-tuple-element.21.own_part, f32[8,128]{1,0:T(8,128)S(1)} %bitcast.7), custom_call_target="tpu_custom_call" | custom-call | flops 1000000 | bytes 1000000 | tf_op jit(solution)/shard_map/pallas_call | solution.py:20
  (1 shorter events, 0.0 us)
Async XLA Ops:
  0.6 9.4 %copy-start = (bf16[32,128,128]{2,1,0:T(8,128)(2,1)S(1)}, bf16[32,128,128]{2,1,0:T(8,128)(2,1)}, u32[]{:S(2)}) copy-start(bf16[32,128,128]{2,1,0:T(8,128)(2,1)} %tiles.3) | copy-start | bytes 3145732
  22.6 1.3 %collective-permute-start = (f32[4,16,128]{2,1,0:T(8,128)S(1)}, f32[4,16,128]{2,1,0:T(8,128)S(1)}, u32[]{:S(2)}, u32[]{:S(2)}) collective-permute-start(f32[4,16,128]{2,1,0:T(8,128)S(1)} %shard_map.88.mine), channel_id=1, source_target_pairs={{0,4},{4,0},{8,12},{12,8},{16,20},{20,16},{24,28},{28,24},{1,5},{5... | collective-permute-start | bytes 98312 | tf_op jit(solution)/shard_map/ppermute | solution.py:226

commit v7 on v5

--- a/solution.py
+++ b/solution.py
@@ -73,7 +73,7 @@
     return one, two, two < FLAG
 
 
-def products(scaled, select, keep, dest_ids, tiles, sources, dest_tiles):
+def products(scaled, select, keep, dest_ids, tiles, sources, dest_tiles, turned=False):
     picked = jnp.dot(select[...], scaled.astype(jnp.bfloat16), preferred_element_type=jnp.float32)
     sources[...] = jnp.where(keep[...] > 0.0, picked, 0.0)
     target = lax.broadcasted_iota(jnp.int32, (dest_tiles, LANES), 0)
@@ -89,8 +89,8 @@
         group = range(first_slot, first_slot + together)
         total += lax.dot_general(
             jnp.concatenate([placed(k) for k in group], axis=1),
-            jnp.concatenate([tiles[k] for k in group], axis=1),
-            (((1,), (1,)), ((), ())),
+            jnp.concatenate([tiles[k] for k in group], axis=0 if turned else 1),
+            (((1,), (0 if turned else 1,)), ((), ())),
             preferred_element_type=jnp.float32,
         )
     return total
@@ -114,8 +114,16 @@
         mine[pair] = damping * total + (1.0 - damping)
 
 
-def second(pages, rows, order, mine, other, got, start, select, keep, dest_ids, tiles, send, own_part, sources):
-    share = got.shape[1] // 2
+def meanwhile(order, got, tiles, weight, flag, turned):
+    _, degree, stuck = unpack(got, order)
+    weight[...] = jnp.where(stuck, 0.0, 1.0 / degree)
+    flag[...] = jnp.where(stuck, 1.0, 0.0)
+    for k in range(tiles.shape[0]):
+        turned[k] = tiles[k].T
+
+
+def second(pages, rows, mine, other, weight, flag, start, select, keep, dest_ids, tiles, send, own_part, sources):
+    share = mine.shape[1]
     b, w = lax.axis_index("blk"), lax.axis_index("row")
     core0 = lax.rem(b, 2) == 0
     pieces = []
@@ -123,10 +131,9 @@
         pieces.append(jnp.where(core0, mine[pair], other[pair]))
         pieces.append(jnp.where(core0, other[pair], mine[pair]))
     rank = jnp.concatenate(pieces, axis=0)
-    _, degree, stuck = unpack(got, order)
-    lost = jnp.sum(jnp.where(stuck, rank, 0.0))
-    scaled = rank * jnp.where(stuck, 0.0, 1.0 / degree)
-    total = products(scaled, select, keep, dest_ids, tiles, sources, rows * share)
+    lost = jnp.sum(rank * flag[...])
+    scaled = rank * weight[...]
+    total = products(scaled, select, keep, dest_ids, tiles, sources, rows * share, turned=True)
     total = damping * (total + lost / pages)
     own = mine[lax.div(b, 2)]
     change = jnp.sum(jnp.abs(own - start[...]))
@@ -170,7 +177,7 @@
     blocks, rows = lax.axis_size("blk"), lax.axis_size("row")
     dest_tiles = rows * share
     by_block = list(range(blocks))[::-1]
-    by_row = [rows // 2] + [w for w in range(rows) if w != rows // 2]
+    by_row = [*range(rows // 2, rows), *range(rows // 2)[::-1]]
     members = [(pair, w) for w in by_row for pair in range(blocks // 2)[::-1]]
     pages = float(blocks * rows * share * LANES)
     f32 = functools.partial(jax.ShapeDtypeStruct, dtype=jnp.float32)
@@ -201,11 +208,15 @@
     got_b = lax.all_to_all(send, ("blk", "row"), 0, 0, axis_index_groups=groups)
     mine = call(functools.partial(gather_rows, rows, members), f32((blocks // 2, share, LANES)))(got_b)
     other = lax.ppermute(mine, "blk", [(i, i ^ 1) for i in range(blocks)])
+    weight, flag, turned = call(
+        functools.partial(meanwhile, by_block),
+        (f32((blocks * share, LANES)), f32((blocks * share, LANES)), jax.ShapeDtypeStruct(tiles.shape, tiles.dtype)),
+    )(got_a, tiles)
     send, own_part = call(
-        functools.partial(second, pages, rows, by_block),
+        functools.partial(second, pages, rows),
         (f32((rows, dest_tiles + SCALAR_ROWS, LANES)), f32((share, LANES))),
         sources,
-    )(mine, other, got_a, start, *table)
+    )(mine, other, weight, flag, start, *table[:3], turned)
 
     got_d = lax.all_to_all(send, "row", 0, 0, axis_index_groups=[by_row])
     send = call(block_change, f32((blocks, LANES)))(got_d)

time: 39.7 us -> 39.3 us (0.990)
    pallas_call x6 -> x7, Pallas kernels: 2.94 us -> 3.09 us  [run(): pl.pallas_call(kernel, out_shape=outs, in_specs=(space,) * len(arguments)...]
  transfers between devices with their start and end apart: 1 -> 1, of which waited for: 1 -> 1; matrix products, arithmetic and copies ran while one was open for 0% -> 0% of each run, Pallas kernels for 0% -> 1%
where the time goes in v7:
time: 39.3 us; the launch traced here: 39 us
  blocking collectives  34.3 us (87%)
  Pallas kernels  3.09 us (8%)
  waiting for transfers between devices  0.86 us (2%)
  between operations  0.68 us (2%)
    all_to_all x1, blocking collectives, local(): got_b = lax.all_to_all(send, ('blk', 'row'), 0, 0, axis_index_groups=groups)  11.1 us
    all_to_all x1, blocking collectives, local(): got_d = lax.all_to_all(send, 'row', 0, 0, axis_index_groups=[by_row])  8.57 us
    all_to_all x1, blocking collectives, local(): got_a = lax.all_to_all(payload, 'blk', 0, 0, axis_index_groups=[by_block])  8.39 us
    all_to_all x1, blocking collectives, local(): lax.all_to_all(send, 'blk', 0, 0, tiled=True, axis_index_groups=[by_block])  6.23 us
    pallas_call x7, Pallas kernels, run(): pl.pallas_call(kernel, out_shape=outs, in_specs=(space,) * len(arguments)...  3.09 us
    ppermute x1, waiting for transfers between devices, local(): other = lax.ppermute(mine, 'blk', [(i, i ^ 1) for i in range(blocks)])  0.86 us
  transfers between devices with their start and end apart: 1, of which 1 were waited for; matrix products, arithmetic and copies ran while one was open for 0% of the time, Pallas kernels for 1%

profile of v7, /device:TPU:0, one launch (start us, length us, event | category | flops | bytes accessed | tf_op | source)
XLA Modules:
  0.0 39.0 jit_solution(5918728171788422112)
XLA Ops:
  0.6 0.0 copy-start
  0.6 1.0 %shard_map.86 = (bf16[8,32,128]{2,1,0:T(8,128)(2,1)S(1)}, bf16[32,128]{1,0:T(8,128)(2,1)S(1)}, f32[32,128]{1,0:T(8,128)S(1)}, s32[32,128]{1,0:T(8,128)S(1)}, f32[16,128]{1,0:T(8,128)S(1)}) custom-call(f32[16,128]{1,0:T(8,128)} %refs_0_.1, s32[16,128]{1,0:T(8,128)} %refs_1_.1, s32[16,128]{1,0:T(8,128)} %refs_2_.1, s32[1,32]{1,0:T(1,128)} %bitcast.9, ...), custom_call_target="tpu_custom_call" | custom-call | flops 1000000000 | bytes 1000000 | tf_op jit(solution)/shard_map/pallas_call | solution.py:20
  1.6 8.4 %all_to_all.26.got = bf16[8,32,128]{2,1,0:T(8,128)(2,1)S(1)} all-to-all(bf16[8,32,128]{2,1,0:T(8,128)(2,1)S(1)} %get-tuple-element.12), channel_id=1, replica_groups={{28,24,20,16,12,8,4,0},{29,25,21,17,13,9,5,1},{30,26,22,18,14,10,6,2},{..., dimensions={0} | all-to-all | bytes 131072 | tf_op jit(solution)/shard_map/all_to_all | solution.py:201
  10.0 0.0 copy-done
  10.0 0.6 %shard_map.87 = f32[16,16,128]{2,1,0:T(8,128)S(1)} custom-call(bf16[8,32,128]{2,1,0:T(8,128)(2,1)S(1)} %all_to_all.26.got, bf16[32,128]{1,0:T(8,128)(2,1)S(1)} %get-tuple-element.13.select, f32[32,128]{1,0:T(8,128)S(1)} %get-tuple-element.14.keep, s32[32,128]{1,0:T(8,128)S(1)} %get-tuple-element.15.dest_ids, bf16[32,128,128]{2,1,0:T(8,128)(2,1)S(1)} %copy-done), custom_call_target="tpu_custom_call" | custom-call | flops 1000000 | bytes 1000000 | tf_op jit(solution)/shard_map/pallas_call | solution.py:20
  10.6 11.1 %all_to_all.27.got = f32[16,16,128]{2,1,0:T(8,128)S(1)} all-to-all(f32[16,16,128]{2,1,0:T(8,128)S(1)} %shard_map.87), channel_id=1, replica_groups={{26,18,10,2,27,19,11,3,25,17,9,1,24,16,8,0},{30,22,14,6,31,23,15,7,29,2..., dimensions={0} | all-to-all | bytes 262144 | tf_op jit(solution)/shard_map/all_to_all | solution.py:208
  21.8 0.1 collective-permute-start
  21.8 0.3 shard_map.89
  22.2 0.9 %collective-permute-done.other = f32[4,16,128]{2,1,0:T(8,128)S(1)} collective-permute-done((f32[4,16,128]{2,1,0:T(8,128)S(1)}, f32[4,16,128]{2,1,0:T(8,128)S(1)}, u32[]{:S(2)}, u32[]{:S(2)}) %collective-permute-start) | collective-permute-done | bytes 32800 | tf_op jit(solution)/shard_map/ppermute | solution.py:210
  23.0 0.4 %shard_map.90 = (f32[4,72,128]{2,1,0:T(8,128)S(1)}, f32[16,128]{1,0:T(8,128)S(1)}) custom-call(f32[4,16,128]{2,1,0:T(8,128)S(1)} %shard_map.88.mine, f32[4,16,128]{2,1,0:T(8,128)S(1)} %collective-permute-done.other, f32[128,128]{1,0:T(8,128)S(1)} %get-tuple-element.16.weight, f32[128,128]{1,0:T(8,128)S(1)} %get-tuple-element.17.flag, ...), custom_call_target="tpu_custom_call" | custom-call | flops 1000000 | bytes 1000000 | tf_op jit(solution)/shard_map/pallas_call | solution.py:20
  23.5 8.6 %all_to_all.28.got = f32[4,72,128]{2,1,0:T(8,128)S(1)} all-to-all(f32[4,72,128]{2,1,0:T(8,128)S(1)} %get-tuple-element.20), channel_id=1, replica_groups={{2,3,1,0},{6,7,5,4},{10,11,9,8},{14,15,13,12},{18,19,17,16},{22,23,21,2..., dimensions={0} | all-to-all | bytes 294912 | tf_op jit(solution)/shard_map/all_to_all | solution.py:221
  32.1 0.1 shard_map.91
  32.2 6.2 %all_to_all.29 = f32[8,1,128]{2,1,0:T(1,128)S(1)} all-to-all(f32[8,1,128]{2,1,0:T(1,128)S(1)} %bitcast.8), channel_id=1, replica_groups={{28,24,20,16,12,8,4,0},{29,25,21,17,13,9,5,1},{30,26,22,18,14,10,6,2},{..., dimensions={0} | all-to-all | bytes 8192 | tf_op jit(solution)/shard_map/all_to_all | solution.py:224
  38.4 0.6 %shard_map.92 = (f32[16,128]{1,0:T(8,128)}, f32[2]{0:T(128)}) custom-call(f32[4,72,128]{2,1,0:T(8,128)S(1)} %all_to_all.28.got, f32[16,128]{1,0:T(8,128)S(1)} %get-tuple-element.21.own_part, f32[8,128]{1,0:T(8,128)S(1)} %bitcast.7), custom_call_target="tpu_custom_call" | custom-call | flops 1000000 | bytes 1000000 | tf_op jit(solution)/shard_map/pallas_call | solution.py:20
  (1 shorter events, 0.0 us)
Async XLA Ops:
  0.6 9.4 %copy-start = (bf16[32,128,128]{2,1,0:T(8,128)(2,1)S(1)}, bf16[32,128,128]{2,1,0:T(8,128)(2,1)}, u32[]{:S(2)}) copy-start(bf16[32,128,128]{2,1,0:T(8,128)(2,1)} %tiles.3) | copy-start | bytes 3145732
  21.8 1.3 %collective-permute-start = (f32[4,16,128]{2,1,0:T(8,128)S(1)}, f32[4,16,128]{2,1,0:T(8,128)S(1)}, u32[]{:S(2)}, u32[]{:S(2)}) collective-permute-start(f32[4,16,128]{2,1,0:T(8,128)S(1)} %shard_map.88.mine), channel_id=1, source_target_pairs={{0,4},{4,0},{8,12},{12,8},{16,20},{20,16},{24,28},{28,24},{1,5},{5... | collective-permute-start | bytes 98312 | tf_op jit(solution)/shard_map/ppermute | solution.py:210

commit v8 on v7

--- a/solution.py
+++ b/solution.py
@@ -13,15 +13,16 @@
 damping = 0.85
 VMEM = pl.BlockSpec(memory_space=pltpu.VMEM)
 HBM = pl.BlockSpec(memory_space=pltpu.HBM)
-
-
-def call(kernel, outs, scratch=(), space=VMEM, flops=1000000):
+SMEM = pl.BlockSpec(memory_space=pltpu.SMEM)
+
+
+def call(kernel, outs, scratch=(), space=VMEM, flops=1000000, scalars=(), scalar_outs=()):
     def run(*arguments):
         return pl.pallas_call(
             kernel,
             out_shape=outs,
-            in_specs=(space,) * len(arguments),
-            out_specs=(VMEM,) * len(outs) if isinstance(outs, tuple) else VMEM,
+            in_specs=[SMEM if i in scalars else space for i in range(len(arguments))],
+            out_specs=tuple(SMEM if i in scalar_outs else VMEM for i in range(len(outs))) if isinstance(outs, tuple) else VMEM,
             scratch_shapes=scratch,
             compiler_params=pltpu.CompilerParams(vmem_limit_bytes=24 * 1024 * 1024),
             cost_estimate=pl.CostEstimate(flops=flops, bytes_accessed=1000000, transcendentals=0),
@@ -30,39 +31,25 @@
     return run
 
 
-def column(row):
-    n = row.shape[1]
-    square = jnp.broadcast_to(row.astype(jnp.float32), (n, n))
-    diagonal = lax.broadcasted_iota(jnp.int32, (n, n), 0) == lax.broadcasted_iota(jnp.int32, (n, n), 1)
-    return jnp.sum(jnp.where(diagonal, square, 0.0), axis=1, keepdims=True)
-
-
 def prepare(*refs):
-    arguments, (payload, select, keep, dest_ids, start), scratch, sems = refs[:6], refs[6:11], refs[11:17], refs[17]
+    arguments, (payload, start, dest, src, fill), (degree, dangling, sems) = refs[:6], refs[6:11], refs[11:]
     copies = [
         pltpu.make_async_copy(source, target, sems.at[i])
-        for i, (source, target) in enumerate(zip(arguments, scratch, strict=True))
+        for i, (source, target) in enumerate(zip(arguments, (start, degree, dangling, dest, src, fill), strict=True))
     ]
     for copy in copies:
         copy.start()
     for copy in copies:
         copy.wait()
-    rank, degree, dangling, dest, src, fill = scratch
-    share = rank.shape[0]
+    share = start.shape[0]
     stuck = dangling[...] > 0
-    degree, rank = degree[...].astype(jnp.float32), rank[...]
+    degree, rank = degree[...].astype(jnp.float32), start[...]
     scaled = (rank * (1.0 / degree)).astype(jnp.bfloat16).astype(jnp.float32)
     high = rank.astype(jnp.bfloat16).astype(jnp.float32)
     planes = [jnp.where(stuck, high, scaled), jnp.where(stuck, rank - high, degree)]
     for i, plane in enumerate(planes):
         rows = slice(i * share, (i + 1) * share)
         payload[:, rows] = jnp.broadcast_to(plane.astype(jnp.bfloat16)[None], (payload.shape[0], share, LANES))
-    start[...] = rank
-    lane = lax.broadcasted_iota(jnp.int32, select.shape, 1).astype(jnp.float32)
-    select[...] = jnp.where(column(src[...]) == lane, 1.0, 0.0).astype(jnp.bfloat16)
-    lane = lax.broadcasted_iota(jnp.int32, keep.shape, 1).astype(jnp.float32)
-    keep[...] = jnp.where(lane < column(fill[...]), 1.0, 0.0)
-    dest_ids[...] = jnp.broadcast_to(column(dest[...]), dest_ids.shape).astype(jnp.int32)
 
 
 def unpack(got, order):
@@ -73,17 +60,17 @@
     return one, two, two < FLAG
 
 
-def products(scaled, select, keep, dest_ids, tiles, sources, dest_tiles, turned=False):
-    picked = jnp.dot(select[...], scaled.astype(jnp.bfloat16), preferred_element_type=jnp.float32)
-    sources[...] = jnp.where(keep[...] > 0.0, picked, 0.0)
+def products(scaled, dest, src, fill, tiles, pages_read, dest_tiles, turned=False):
+    pages_read[...] = scaled.astype(jnp.bfloat16).astype(jnp.float32)
     target = lax.broadcasted_iota(jnp.int32, (dest_tiles, LANES), 0)
+    lane = lax.broadcasted_iota(jnp.int32, (1, LANES), 1)
     total = jnp.zeros((dest_tiles, LANES), jnp.float32)
     slots = tiles.shape[0]
     together = 2 - slots % 2
 
     def placed(k):
-        line = jnp.where(dest_ids[pl.ds(k, 1), :] == target, sources[pl.ds(k, 1), :], 0.0)
-        return line.astype(jnp.bfloat16)
+        source = jnp.where(lane < fill[0, k], pages_read[pl.ds(src[0, k], 1), :], 0.0)
+        return jnp.where(target == dest[0, k], source, 0.0).astype(jnp.bfloat16)
 
     for first_slot in range(0, slots, together):
         group = range(first_slot, first_slot + together)
@@ -96,12 +83,12 @@
     return total
 
 
-def first(pages, rows, order, members, got, select, keep, dest_ids, tiles, send, sources):
+def first(pages, rows, order, members, got, dest, src, fill, tiles, send, pages_read):
     share = got.shape[1] // 2
     one, two, stuck = unpack(got, order)
     lost = jnp.sum(jnp.where(stuck, one + two, 0.0))
     scaled = jnp.where(stuck, 0.0, one)
-    total = products(scaled, select, keep, dest_ids, tiles, sources, rows * share) + lost / pages
+    total = products(scaled, dest, src, fill, tiles, pages_read, rows * share) + lost / pages
     for i, (_, w) in enumerate(members):
         send[i] = total[w * share : (w + 1) * share]
 
@@ -122,7 +109,7 @@
         turned[k] = tiles[k].T
 
 
-def second(pages, rows, mine, other, weight, flag, start, select, keep, dest_ids, tiles, send, own_part, sources):
+def second(pages, rows, mine, other, weight, flag, start, dest, src, fill, tiles, send, own_part, pages_read):
     share = mine.shape[1]
     b, w = lax.axis_index("blk"), lax.axis_index("row")
     core0 = lax.rem(b, 2) == 0
@@ -133,7 +120,7 @@
     rank = jnp.concatenate(pieces, axis=0)
     lost = jnp.sum(rank * flag[...])
     scaled = rank * weight[...]
-    total = products(scaled, select, keep, dest_ids, tiles, sources, rows * share, turned=True)
+    total = products(scaled, dest, src, fill, tiles, pages_read, rows * share, turned=True)
     total = damping * (total + lost / pages)
     own = mine[lax.div(b, 2)]
     change = jnp.sum(jnp.abs(own - start[...]))
@@ -181,28 +168,27 @@
     members = [(pair, w) for w in by_row for pair in range(blocks // 2)[::-1]]
     pages = float(blocks * rows * share * LANES)
     f32 = functools.partial(jax.ShapeDtypeStruct, dtype=jnp.float32)
-    sources = (pltpu.VMEM((slots, LANES), jnp.float32),)
+    pages_read = (pltpu.VMEM((blocks * share, LANES), jnp.float32),)
 
     arguments = (rank_start, out_degree, dangling, tile_dest[None], tile_src[None], tile_fill[None])
-    payload, *table, start = call(
+    whole, line = (share, LANES), pltpu.SMEM((1, slots), jnp.int32)
+    payload, start, *table = call(
         prepare,
-        (
-            jax.ShapeDtypeStruct((blocks, 2 * share, LANES), jnp.bfloat16),
-            jax.ShapeDtypeStruct((slots, blocks * share), jnp.bfloat16),
-            f32((slots, LANES)),
-            jax.ShapeDtypeStruct((slots, LANES), jnp.int32),
-            f32((share, LANES)),
-        ),
-        (*(pltpu.VMEM(a.shape, a.dtype) for a in arguments), pltpu.SemaphoreType.DMA((len(arguments),))),
+        (jax.ShapeDtypeStruct((blocks, 2 * share, LANES), jnp.bfloat16), f32(whole), line, line, line),
+        (pltpu.VMEM(whole, jnp.int32), pltpu.VMEM(whole, jnp.int32), pltpu.SemaphoreType.DMA((len(arguments),))),
         HBM,
         flops=1000000000,
+        scalar_outs=(2, 3, 4),
     )(*(pltpu.with_memory_space_constraint(a, pltpu.HBM) for a in arguments))
+    table = [pltpu.with_memory_space_constraint(a, pltpu.SMEM) for a in table]
 
     got_a = lax.all_to_all(payload, "blk", 0, 0, axis_index_groups=[by_block])
-    table = (*table, tiles)
-    send = call(functools.partial(first, pages, rows, by_block, members), f32((len(members), share, LANES)), sources)(
-        got_a, *table
-    )
+    send = call(
+        functools.partial(first, pages, rows, by_block, members),
+        f32((len(members), share, LANES)),
+        pages_read,
+        scalars=(1, 2, 3),
+    )(got_a, *table, tiles)
 
     groups = [[(2 * pair + core) * rows + w for pair, w in members] for core in range(2)]
     got_b = lax.all_to_all(send, ("blk", "row"), 0, 0, axis_index_groups=groups)
@@ -215,8 +201,9 @@
     send, own_part = call(
         functools.partial(second, pages, rows),
         (f32((rows, dest_tiles + SCALAR_ROWS, LANES)), f32((share, LANES))),
-        sources,
-    )(mine, other, weight, flag, start, *table[:3], turned)
+        pages_read,
+        scalars=(5, 6, 7),
+    )(mine, other, weight, flag, start, *table, turned)
 
     got_d = lax.all_to_all(send, "row", 0, 0, axis_index_groups=[by_row])
     send = call(block_change, f32((blocks, LANES)))(got_d)

time: 39.3 us -> 39.1 us (level)
  no operation moved by 1% of the time
where the time goes in v8:
time: 39.1 us; the launch traced here: 38.8 us
  blocking collectives  34.3 us (88%)
  Pallas kernels  2.83 us (7%)
  waiting for transfers between devices  0.86 us (2%)
  between operations  0.69 us (2%)
    all_to_all x1, blocking collectives, local(): got_b = lax.all_to_all(send, ('blk', 'row'), 0, 0, axis_index_groups=groups)  11.1 us
    all_to_all x1, blocking collectives, local(): got_d = lax.all_to_all(send, 'row', 0, 0, axis_index_groups=[by_row])  8.57 us
    all_to_all x1, blocking collectives, local(): got_a = lax.all_to_all(payload, 'blk', 0, 0, axis_index_groups=[by_block])  8.39 us
    all_to_all x1, blocking collectives, local(): lax.all_to_all(send, 'blk', 0, 0, tiled=True, axis_index_groups=[by_block])  6.23 us
    pallas_call x7, Pallas kernels, run(): pl.pallas_call(kernel, out_shape=outs, in_specs=[SMEM if i in scalars els...  2.83 us
    ppermute x1, waiting for transfers between devices, local(): other = lax.ppermute(mine, 'blk', [(i, i ^ 1) for i in range(blocks)])  0.86 us
  transfers between devices with their start and end apart: 1, of which 1 were waited for; matrix products, arithmetic and copies ran while one was open for 0% of the time, Pallas kernels for 1%

profile of v8, /device:TPU:0, one launch (start us, length us, event | category | flops | bytes accessed | tf_op | source)
XLA Modules:
  0.0 38.8 jit_solution(7822676559775847871)
XLA Ops:
  0.6 0.0 copy-start
  0.6 0.9 %shard_map.86 = (bf16[8,32,128]{2,1,0:T(8,128)(2,1)S(1)}, f32[16,128]{1,0:T(8,128)S(1)}, s32[1,32]{1,0:T(1,128)S(4)}, s32[1,32]{1,0:T(1,128)S(4)}, s32[1,32]{1,0:T(1,128)S(4)}) custom-call(f32[16,128]{1,0:T(8,128)} %refs_0_.1, s32[16,128]{1,0:T(8,128)} %refs_1_.1, s32[16,128]{1,0:T(8,128)} %refs_2_.1, s32[1,32]{1,0:T(1,128)} %bitcast.9, s32[1,32]{1,0:T(1,128)} %bitcast.10, ...), custom_call_target="tpu_custom_call" | custom-call | flops 1000000000 | bytes 1000000 | tf_op jit(solution)/shard_map/pallas_call | solution.py:21
  1.6 8.4 %all_to_all.26.got = bf16[8,32,128]{2,1,0:T(8,128)(2,1)S(1)} all-to-all(bf16[8,32,128]{2,1,0:T(8,128)(2,1)S(1)} %get-tuple-element.12), channel_id=1, replica_groups={{28,24,20,16,12,8,4,0},{29,25,21,17,13,9,5,1},{30,26,22,18,14,10,6,2},{..., dimensions={0} | all-to-all | bytes 131072 | tf_op jit(solution)/shard_map/all_to_all | solution.py:185
  9.9 0.0 copy-done
  10.0 0.5 %shard_map.87 = f32[16,16,128]{2,1,0:T(8,128)S(1)} custom-call(bf16[8,32,128]{2,1,0:T(8,128)(2,1)S(1)} %all_to_all.26.got, s32[1,32]{1,0:T(1,128)S(4)} %get-tuple-element.13.dest, s32[1,32]{1,0:T(1,128)S(4)} %get-tuple-element.14.src, s32[1,32]{1,0:T(1,128)S(4)} %get-tuple-element.15.fill, bf16[32,128,128]{2,1,0:T(8,128)(2,1)S(1)} %copy-done), custom_call_target="tpu_custom_call" | custom-call | flops 1000000 | bytes 1000000 | tf_op jit(solution)/shard_map/pallas_call | solution.py:21
  10.4 11.1 %all_to_all.27.got = f32[16,16,128]{2,1,0:T(8,128)S(1)} all-to-all(f32[16,16,128]{2,1,0:T(8,128)S(1)} %shard_map.87), channel_id=1, replica_groups={{26,18,10,2,27,19,11,3,25,17,9,1,24,16,8,0},{30,22,14,6,31,23,15,7,29,2..., dimensions={0} | all-to-all | bytes 262144 | tf_op jit(solution)/shard_map/all_to_all | solution.py:194
  21.6 0.1 collective-permute-start
  21.7 0.3 shard_map.89
  22.0 0.9 %collective-permute-done.other = f32[4,16,128]{2,1,0:T(8,128)S(1)} collective-permute-done((f32[4,16,128]{2,1,0:T(8,128)S(1)}, f32[4,16,128]{2,1,0:T(8,128)S(1)}, u32[]{:S(2)}, u32[]{:S(2)}) %collective-permute-start) | collective-permute-done | bytes 32800 | tf_op jit(solution)/shard_map/ppermute | solution.py:196
  22.9 0.4 shard_map.90
  23.2 8.6 %all_to_all.28.got = f32[4,72,128]{2,1,0:T(8,128)S(1)} all-to-all(f32[4,72,128]{2,1,0:T(8,128)S(1)} %get-tuple-element.20), channel_id=1, replica_groups={{2,3,1,0},{6,7,5,4},{10,11,9,8},{14,15,13,12},{18,19,17,16},{22,23,21,2..., dimensions={0} | all-to-all | bytes 294912 | tf_op jit(solution)/shard_map/all_to_all | solution.py:208
  31.8 0.1 shard_map.91
  31.9 6.2 %all_to_all.29 = f32[8,1,128]{2,1,0:T(1,128)S(1)} all-to-all(f32[8,1,128]{2,1,0:T(1,128)S(1)} %bitcast.8), channel_id=1, replica_groups={{28,24,20,16,12,8,4,0},{29,25,21,17,13,9,5,1},{30,26,22,18,14,10,6,2},{..., dimensions={0} | all-to-all | bytes 8192 | tf_op jit(solution)/shard_map/all_to_all | solution.py:211
  38.2 0.6 %shard_map.92 = (f32[16,128]{1,0:T(8,128)}, f32[2]{0:T(128)}) custom-call(f32[4,72,128]{2,1,0:T(8,128)S(1)} %all_to_all.28.got, f32[16,128]{1,0:T(8,128)S(1)} %get-tuple-element.21.own_part, f32[8,128]{1,0:T(8,128)S(1)} %bitcast.7), custom_call_target="tpu_custom_call" | custom-call | flops 1000000 | bytes 1000000 | tf_op jit(solution)/shard_map/pallas_call | solution.py:21
  (1 shorter events, 0.0 us)
Async XLA Ops:
  0.6 9.3 %copy-start = (bf16[32,128,128]{2,1,0:T(8,128)(2,1)S(1)}, bf16[32,128,128]{2,1,0:T(8,128)(2,1)}, u32[]{:S(2)}) copy-start(bf16[32,128,128]{2,1,0:T(8,128)(2,1)} %tiles.3) | copy-start | bytes 3145732
  21.6 1.3 %collective-permute-start = (f32[4,16,128]{2,1,0:T(8,128)S(1)}, f32[4,16,128]{2,1,0:T(8,128)S(1)}, u32[]{:S(2)}, u32[]{:S(2)}) collective-permute-start(f32[4,16,128]{2,1,0:T(8,128)S(1)} %shard_map.88.mine), channel_id=1, source_target_pairs={{0,4},{4,0},{8,12},{12,8},{16,20},{20,16},{24,28},{28,24},{1,5},{5... | collective-permute-start | bytes 98312 | tf_op jit(solution)/shard_map/ppermute | solution.py:196
